TPU v7x, 32 devices: a whole 2x2x4 slice. The times are simulated.
32 devices in a mesh: gx: 4 (over y, core), gy: 4 (over z), gz: 2 (over x).
Axes of the slice: x: 2, y: 2, z: 4, core: 2. Of those that a mesh axis runs over, the one named last changes fastest.
Arguments:
- spin_vectors: float32 [2, 3, 32, 32, 256], P(None, None, 'gx', 'gy', 'gz'), may hold values from -1 to 1, as said below
- displacement: float32 [2, 3, 32, 32, 256], P(None, None, 'gx', 'gy', 'gz'), may hold values from -0.15 to 0.15
- occupied: int32 [2, 32, 32, 256], P(None, 'gx', 'gy', 'gz'), may hold values 0 or 1
- applied_field: float32 [3], replicated, may hold values from -4 to 4
Outputs:
- new_spins: float32 [2, 3, 32, 32, 256], P(None, None, 'gx', 'gy', 'gz')
- forces: float32 [2, 3, 32, 32, 256], P(None, None, 'gx', 'gy', 'gz')
Inputs may be any that keep to these rules, and one draw needn't show every extreme that they name: `occupied`: 1 where a lattice site holds an atom, 0 at a vacancy. `spin_vectors`: every spin vector has unit length.
All inputs are finite; a program needn't handle non-finite values. No bound on the sum of `occupied` on one device may be relied on, other than what follows from the above.
Results may differ from a plain program's by a relative error of at most 0.0001.
Values sent between devices are 32-bit elements; how exact they have to be, the bound alone decides.
A program may use at most 64 MiB of HBM per device.

v0:
```python
import jax
import jax.numpy as jnp
from jax import lax
from jax.sharding import PartitionSpec as P

step_time = 0.6
exchange_scale = 0.35
exchange_decay = 4.0
pair_scale = 0.5
pair_decay = 6.0
density_decay = 3.0
bond_length = 0.8660254037844386
corner_offsets = [(a, b, c) for a in (0, 1) for b in (0, 1) for c in (0, 1)]


def shifted(block, axis, distance):
    devices = range(lax.axis_size(axis))
    route = [((i - distance) % len(devices), i) for i in devices]
    return lax.ppermute(block, axis, route)


def padded_2(value, sides, width):
    for axis, dim in sides:
        count, length = (lax.axis_size(axis), value.shape[dim])
        up = [(i, (i + 1) % count) for i in range(count)]
        down = [(j, i) for i, j in up]
        last = lax.slice_in_dim(value, length - width, length, axis=dim)
        initial = lax.slice_in_dim(value, 0, width, axis=dim)
        before = lax.ppermute(last, axis, up)
        after = lax.ppermute(initial, axis, down)
        value = jnp.concatenate([before, value, after], axis=dim)
    return value


def window_of(values, anchor, lowest, margin, counts):
    leading = values.ndim - 3
    starts = [0] * leading + [lowest[i] - anchor for i in range(3)]
    limits = list(values.shape[:leading]) + [
        starts[leading + i] + counts[i] + margin for i in range(3)
    ]
    return lax.slice(values, starts, limits)


def cross_product(left, right):
    return jnp.stack(
        [
            left[1] * right[2] - left[2] * right[1],
            left[2] * right[0] - left[0] * right[2],
            left[0] * right[1] - left[1] * right[0],
        ]
    )


def rotate(spin_state, torque, fraction):
    rotation = 0.5 * fraction * torque
    first_turn = cross_product(rotation, spin_state)
    second_turn = cross_product(rotation, first_turn)
    factor = 2.0 / (1.0 + jnp.sum(rotation * rotation, axis=0))
    return spin_state + factor * (first_turn + second_turn)


def bond_terms(padded, halo_depth, lowest, margin, counts):
    vectors, lengths, weights = ([], [], [])
    owners = window_of(padded, -halo_depth, (lowest, lowest, lowest), margin, counts)
    for offset in corner_offsets:
        partner = window_of(
            padded, -halo_depth, tuple((lowest - o for o in offset)), margin, counts
        )
        vector = jnp.stack([0.5 - offset[i] + partner[3 + i] - owners[i] for i in range(3)])
        vectors.append(vector)
        lengths.append(jnp.sqrt(jnp.sum(vector * vector, axis=0)))
        weights.append(owners[6] * partner[7])
    return (jnp.stack(vectors), jnp.stack(lengths), jnp.stack(weights))


def first_field(coupling, ghosts, lowest, counts, external):
    summed = external
    for corner, offset in enumerate(corner_offsets):
        bond_term = window_of(coupling[corner], lowest, (0, 0, 0), 0, counts)
        partner = window_of(ghosts[1], -1, tuple((-o for o in offset)), 0, counts)
        summed = summed + bond_term[None] * partner
    return summed


def second_field(coupling, ghosts, lowest, counts, external):
    summed = external
    for corner, offset in enumerate(corner_offsets):
        bond_term = window_of(coupling[corner], lowest, offset, 0, counts)
        partner = window_of(ghosts[0], -1, offset, 0, counts)
        summed = summed + bond_term[None] * partner
    return summed


def send_upper(turned):
    extended = jnp.concatenate([turned, shifted(turned[:, :1], "gx", -1)], axis=1)
    extended = jnp.concatenate([extended, shifted(extended[:, :, :1], "gy", -1)], axis=2)
    return jnp.concatenate([extended, shifted(extended[:, :, :, :1], "gz", -1)], axis=3)


def send_lower(turned):
    extended = jnp.concatenate([shifted(turned[:, -1:], "gx", 1), turned], axis=1)
    extended = jnp.concatenate([shifted(extended[:, :, -1:], "gy", 1), extended], axis=2)
    return jnp.concatenate([shifted(extended[:, :, :, -1:], "gz", 1), extended], axis=3)


def on_device(spin_vectors, displacement, occupied, applied_field):
    counts = spin_vectors.shape[2:]
    placed = jnp.concatenate(
        [displacement.reshape((6,) + counts), occupied.astype(jnp.float32)], axis=0
    )
    halo_depth = 1
    padded = padded_2(placed, (("gx", 1), ("gy", 2), ("gz", 3)), 1)
    lowest = 1 - halo_depth
    margin = 2 * halo_depth - 1
    vectors, lengths, weights = bond_terms(padded, halo_depth, lowest, margin, counts)
    stretch = lengths - bond_length
    coupling = weights * exchange_scale * jnp.exp(-exchange_decay * stretch)
    density = weights * jnp.exp(-density_decay * stretch)
    external = applied_field[:, None, None, None]
    x_half = (lax.broadcasted_iota(jnp.int32, counts, 0) >= counts[0] // 2).astype(jnp.int32)
    y_half = (lax.broadcasted_iota(jnp.int32, counts, 1) >= counts[1] // 2).astype(jnp.int32)
    spin_pad = jnp.zeros((2, 3) + tuple((c + 2 for c in counts)), jnp.float32)
    spin_pad = spin_pad.at[1, :, :-1, :-1, :-1].set(send_lower(spin_vectors[1]))

    def sector_turn(update_index, torque, chosen):
        sector = jnp.where(update_index < 8, update_index, 14 - update_index)
        quarter = sector // 2
        fraction = jnp.where(update_index == 7, step_time, 0.5 * step_time)
        turned = rotate(chosen, torque, fraction)
        inside = (x_half == quarter % 2) & (y_half == quarter // 2)
        return jnp.where(inside[None], turned, chosen)

    def lower_update(update_index, state):
        own_spins, ghosts = state
        torque = first_field(coupling, ghosts, lowest, counts, external)
        turned = sector_turn(update_index, torque, own_spins[0])
        own_spins = own_spins.at[0].set(turned)
        ghosts = ghosts.at[0, :, 1:, 1:, 1:].set(send_upper(turned))
        return (own_spins, ghosts)

    def upper_update(update_index, state):
        own_spins, ghosts = state
        torque = second_field(coupling, ghosts, lowest, counts, external)
        turned = sector_turn(update_index, torque, own_spins[1])
        own_spins = own_spins.at[1].set(turned)
        ghosts = ghosts.at[1, :, :-1, :-1, :-1].set(send_lower(turned))
        return (own_spins, ghosts)

    def pair_step(pair_index, state):
        state = lower_update(2 * pair_index, state)
        return upper_update(2 * pair_index + 1, state)

    state = lax.fori_loop(0, 7, pair_step, (spin_vectors, spin_pad))
    own_spins, spin_pad = lower_update(14, state)
    first_density = sum(
        (window_of(density[corner], lowest, (0, 0, 0), 0, counts) for corner in range(8))
    )
    second_density = sum(
        (
            window_of(density[corner], lowest, corner_offsets[corner], 0, counts)
            for corner in range(8)
        )
    )
    own_slope = -0.5 / jnp.sqrt(1.0 + jnp.stack([first_density, second_density]))
    embed_slope = padded_2(own_slope, (("gx", 1), ("gy", 2), ("gz", 3)), 1)
    first_force = jnp.zeros((3,) + counts, jnp.float32)
    second_force = jnp.zeros((3,) + counts, jnp.float32)
    for corner, offset in enumerate(corner_offsets):
        backward = tuple((-o for o in offset))
        bond_stretch = window_of(stretch[corner], lowest, (0, 0, 0), 1, counts)
        bond_weight = window_of(weights[corner], lowest, (0, 0, 0), 1, counts)
        bond_coupling = window_of(coupling[corner], lowest, (0, 0, 0), 1, counts)
        bond_vector = window_of(vectors[corner], lowest, (0, 0, 0), 1, counts)
        bond_length_here = window_of(lengths[corner], lowest, (0, 0, 0), 1, counts)
        alignment = jnp.sum(
            window_of(spin_pad[0], -1, (0, 0, 0), 1, counts)
            * window_of(spin_pad[1], -1, backward, 1, counts),
            axis=0,
        )
        slopes = window_of(embed_slope[0], -1, (0, 0, 0), 1, counts) + window_of(
            embed_slope[1], -1, backward, 1, counts
        )
        strength = (
            -pair_decay * pair_scale * bond_weight * jnp.exp(-pair_decay * bond_stretch)
            - density_decay * bond_weight * jnp.exp(-density_decay * bond_stretch) * slopes
            + exchange_decay * bond_coupling * alignment
        )
        bond_force = strength[None] * bond_vector / bond_length_here[None]
        first_force = first_force + window_of(bond_force, 0, (0, 0, 0), 0, counts)
        second_force = second_force - window_of(bond_force, 0, offset, 0, counts)
    return (own_spins, jnp.stack([first_force, second_force]))


def solution(mesh):
    placed = (
        P(None, None, "gx", "gy", "gz"),
        P(None, None, "gx", "gy", "gz"),
        P(None, "gx", "gy", "gz"),
        P(),
    )
    return jax.shard_map(
        on_device,
        mesh=mesh,
        in_specs=placed,
        out_specs=(P(None, None, "gx", "gy", "gz"), P(None, None, "gx", "gy", "gz")),
        check_vma=False,
    )
```

profile of v0, /device:TPU:1, one launch (start us, length us, event | category | flops | bytes accessed | tf_op | source)
XLA Modules:
  0.0 454.2 jit_solution(8784935352170859021)
XLA Ops:
  29.4 366.4 %while.28 = (s32[]{:T(128)}, f32[2,3,8,8,128]{4,3,2,1,0:T(8,128)S(1)}, f32[2,3,10,10,130]{4,3,2,1,0:T(8,128)S(1)}, f32[3,1,1,1]{0,3,2,1:T(1,128)S(1)}, f32[8,9,9...) while((s32[]{:T(128)}, ...), condition=%wide.region_11.12_spmd.clone.clone.clone, body=%wide.region_8.11_spmd.clone.clone.clone.sunk | while | flops 2244082 | bytes 10255335 | solution.py:153
  44.8 6.3 %collective-permute-done.2 = f32[3,9,9,1]{3,2,1,0:T(8,128)S(1)} collective-permute-done((f32[3,9,9,1]{3,2,1,0:T(8,128)S(1)}, f32[3,9,9,1]{3,2,1,0:T(8,128)S(1)}, u32[]{:S(2)}, u32[]{:S(2)}) %collective-permute-start.2) | collective-permute-done | bytes 1004 | tf_op jit(solution)/shard_map/while/body/eval_jaxpr/ppermute | solution.py:19
  51.1 13.3 %scatter.59 = f32[2,3,10,10,130]{4,3,2,1,0:T(8,128)S(1)} dynamic-update-slice(f32[2,3,10,10,130]{4,3,2,1,0:T(8,128)S(1)} %get-tuple-element.718, f32[1,3,9,9,129]{4,3,2,1,0:T(8,128)S(1)} %maximum_bitcast_fusion.6, s32[]{:T(128)} %constant.627.clone.1..sunk, s32[]{:T(128)} %constant.627.clone.1..sunk, s32[]{:T(128)} %constant.642.clone.1..sunk, s32[]{:T(128)} %constant.642.clone.1..sunk, ...) | dynamic-update-slice | bytes 250780 | tf_op jit(solution)/shard_map/while/body/eval_jaxpr/scatter | solution.py:138
  67.9 4.7 %collective-permute-done.4 = f32[3,9,1,128]{3,2,1,0:T(1,128)S(1)} collective-permute-done((f32[3,9,1,128]{3,2,1,0:T(1,128)S(1)}, f32[3,9,1,128]{3,2,1,0:T(1,128)S(1)}, u32[]{:S(2)}, u32[]{:S(2)}) %collective-permute-start.4) | collective-permute-done | bytes 13856 | tf_op jit(solution)/shard_map/while/body/eval_jaxpr/ppermute | solution.py:19
  77.8 5.6 %scatter.60 = f32[2,3,10,10,130]{4,3,2,1,0:T(8,128)S(1)} dynamic-update-slice(f32[2,3,10,10,130]{4,3,2,1,0:T(8,128)S(1)} %scatter.59, f32[1,3,9,9,129]{4,3,2,1,0:T(8,128)S(1)} %maximum_bitcast_fusion.7, s32[]{:T(128)} %constant.642.clone.1..sunk, s32[]{:T(128)} %constant.627.clone.1..sunk, s32[]{:T(128)} %constant.627.clone.1..sunk, s32[]{:T(128)} %constant.627.clone.1..sunk, ...) | dynamic-update-slice | bytes 250780 | tf_op jit(solution)/shard_map/while/body/eval_jaxpr/scatter | solution.py:146
  97.2 6.2 %collective-permute-done.2 = f32[3,9,9,1]{3,2,1,0:T(8,128)S(1)} collective-permute-done((f32[3,9,9,1]{3,2,1,0:T(8,128)S(1)}, f32[3,9,9,1]{3,2,1,0:T(8,128)S(1)}, u32[]{:S(2)}, u32[]{:S(2)}) %collective-permute-start.2) | collective-permute-done | bytes 1004 | tf_op jit(solution)/shard_map/while/body/eval_jaxpr/ppermute | solution.py:19
  103.4 13.3 %scatter.59 = f32[2,3,10,10,130]{4,3,2,1,0:T(8,128)S(1)} dynamic-update-slice(f32[2,3,10,10,130]{4,3,2,1,0:T(8,128)S(1)} %get-tuple-element.718, f32[1,3,9,9,129]{4,3,2,1,0:T(8,128)S(1)} %maximum_bitcast_fusion.6, s32[]{:T(128)} %constant.627.clone.1..sunk, s32[]{:T(128)} %constant.627.clone.1..sunk, s32[]{:T(128)} %constant.642.clone.1..sunk, s32[]{:T(128)} %constant.642.clone.1..sunk, ...) | dynamic-update-slice | bytes 250780 | tf_op jit(solution)/shard_map/while/body/eval_jaxpr/scatter | solution.py:138
  129.9 5.6 %scatter.60 = f32[2,3,10,10,130]{4,3,2,1,0:T(8,128)S(1)} dynamic-update-slice(f32[2,3,10,10,130]{4,3,2,1,0:T(8,128)S(1)} %scatter.59, f32[1,3,9,9,129]{4,3,2,1,0:T(8,128)S(1)} %maximum_bitcast_fusion.7, s32[]{:T(128)} %constant.642.clone.1..sunk, s32[]{:T(128)} %constant.627.clone.1..sunk, s32[]{:T(128)} %constant.627.clone.1..sunk, s32[]{:T(128)} %constant.627.clone.1..sunk, ...) | dynamic-update-slice | bytes 250780 | tf_op jit(solution)/shard_map/while/body/eval_jaxpr/scatter | solution.py:146
  149.4 6.2 %collective-permute-done.2 = f32[3,9,9,1]{3,2,1,0:T(8,128)S(1)} collective-permute-done((f32[3,9,9,1]{3,2,1,0:T(8,128)S(1)}, f32[3,9,9,1]{3,2,1,0:T(8,128)S(1)}, u32[]{:S(2)}, u32[]{:S(2)}) %collective-permute-start.2) | collective-permute-done | bytes 1004 | tf_op jit(solution)/shard_map/while/body/eval_jaxpr/ppermute | solution.py:19
  155.6 13.3 %scatter.59 = f32[2,3,10,10,130]{4,3,2,1,0:T(8,128)S(1)} dynamic-update-slice(f32[2,3,10,10,130]{4,3,2,1,0:T(8,128)S(1)} %get-tuple-element.718, f32[1,3,9,9,129]{4,3,2,1,0:T(8,128)S(1)} %maximum_bitcast_fusion.6, s32[]{:T(128)} %constant.627.clone.1..sunk, s32[]{:T(128)} %constant.627.clone.1..sunk, s32[]{:T(128)} %constant.642.clone.1..sunk, s32[]{:T(128)} %constant.642.clone.1..sunk, ...) | dynamic-update-slice | bytes 250780 | tf_op jit(solution)/shard_map/while/body/eval_jaxpr/scatter | solution.py:138
  181.9 5.6 %scatter.60 = f32[2,3,10,10,130]{4,3,2,1,0:T(8,128)S(1)} dynamic-update-slice(f32[2,3,10,10,130]{4,3,2,1,0:T(8,128)S(1)} %scatter.59, f32[1,3,9,9,129]{4,3,2,1,0:T(8,128)S(1)} %maximum_bitcast_fusion.7, s32[]{:T(128)} %constant.642.clone.1..sunk, s32[]{:T(128)} %constant.627.clone.1..sunk, s32[]{:T(128)} %constant.627.clone.1..sunk, s32[]{:T(128)} %constant.627.clone.1..sunk, ...) | dynamic-update-slice | bytes 250780 | tf_op jit(solution)/shard_map/while/body/eval_jaxpr/scatter | solution.py:146
  201.4 6.1 %collective-permute-done.2 = f32[3,9,9,1]{3,2,1,0:T(8,128)S(1)} collective-permute-done((f32[3,9,9,1]{3,2,1,0:T(8,128)S(1)}, f32[3,9,9,1]{3,2,1,0:T(8,128)S(1)}, u32[]{:S(2)}, u32[]{:S(2)}) %collective-permute-start.2) | collective-permute-done | bytes 1004 | tf_op jit(solution)/shard_map/while/body/eval_jaxpr/ppermute | solution.py:19
  207.5 13.3 %scatter.59 = f32[2,3,10,10,130]{4,3,2,1,0:T(8,128)S(1)} dynamic-update-slice(f32[2,3,10,10,130]{4,3,2,1,0:T(8,128)S(1)} %get-tuple-element.718, f32[1,3,9,9,129]{4,3,2,1,0:T(8,128)S(1)} %maximum_bitcast_fusion.6, s32[]{:T(128)} %constant.627.clone.1..sunk, s32[]{:T(128)} %constant.627.clone.1..sunk, s32[]{:T(128)} %constant.642.clone.1..sunk, s32[]{:T(128)} %constant.642.clone.1..sunk, ...) | dynamic-update-slice | bytes 250780 | tf_op jit(solution)/shard_map/while/body/eval_jaxpr/scatter | solution.py:138
  234.0 5.6 %scatter.60 = f32[2,3,10,10,130]{4,3,2,1,0:T(8,128)S(1)} dynamic-update-slice(f32[2,3,10,10,130]{4,3,2,1,0:T(8,128)S(1)} %scatter.59, f32[1,3,9,9,129]{4,3,2,1,0:T(8,128)S(1)} %maximum_bitcast_fusion.7, s32[]{:T(128)} %constant.642.clone.1..sunk, s32[]{:T(128)} %constant.627.clone.1..sunk, s32[]{:T(128)} %constant.627.clone.1..sunk, s32[]{:T(128)} %constant.627.clone.1..sunk, ...) | dynamic-update-slice | bytes 250780 | tf_op jit(solution)/shard_map/while/body/eval_jaxpr/scatter | solution.py:146
  253.6 6.2 %collective-permute-done.2 = f32[3,9,9,1]{3,2,1,0:T(8,128)S(1)} collective-permute-done((f32[3,9,9,1]{3,2,1,0:T(8,128)S(1)}, f32[3,9,9,1]{3,2,1,0:T(8,128)S(1)}, u32[]{:S(2)}, u32[]{:S(2)}) %collective-permute-start.2) | collective-permute-done | bytes 1004 | tf_op jit(solution)/shard_map/while/body/eval_jaxpr/ppermute | solution.py:19
  259.8 13.3 %scatter.59 = f32[2,3,10,10,130]{4,3,2,1,0:T(8,128)S(1)} dynamic-update-slice(f32[2,3,10,10,130]{4,3,2,1,0:T(8,128)S(1)} %get-tuple-element.718, f32[1,3,9,9,129]{4,3,2,1,0:T(8,128)S(1)} %maximum_bitcast_fusion.6, s32[]{:T(128)} %constant.627.clone.1..sunk, s32[]{:T(128)} %constant.627.clone.1..sunk, s32[]{:T(128)} %constant.642.clone.1..sunk, s32[]{:T(128)} %constant.642.clone.1..sunk, ...) | dynamic-update-slice | bytes 250780 | tf_op jit(solution)/shard_map/while/body/eval_jaxpr/scatter | solution.py:138
  286.1 5.6 %scatter.60 = f32[2,3,10,10,130]{4,3,2,1,0:T(8,128)S(1)} dynamic-update-slice(f32[2,3,10,10,130]{4,3,2,1,0:T(8,128)S(1)} %scatter.59, f32[1,3,9,9,129]{4,3,2,1,0:T(8,128)S(1)} %maximum_bitcast_fusion.7, s32[]{:T(128)} %constant.642.clone.1..sunk, s32[]{:T(128)} %constant.627.clone.1..sunk, s32[]{:T(128)} %constant.627.clone.1..sunk, s32[]{:T(128)} %constant.627.clone.1..sunk, ...) | dynamic-update-slice | bytes 250780 | tf_op jit(solution)/shard_map/while/body/eval_jaxpr/scatter | solution.py:146
  305.5 6.1 %collective-permute-done.2 = f32[3,9,9,1]{3,2,1,0:T(8,128)S(1)} collective-permute-done((f32[3,9,9,1]{3,2,1,0:T(8,128)S(1)}, f32[3,9,9,1]{3,2,1,0:T(8,128)S(1)}, u32[]{:S(2)}, u32[]{:S(2)}) %collective-permute-start.2) | collective-permute-done | bytes 1004 | tf_op jit(solution)/shard_map/while/body/eval_jaxpr/ppermute | solution.py:19
  311.6 13.3 %scatter.59 = f32[2,3,10,10,130]{4,3,2,1,0:T(8,128)S(1)} dynamic-update-slice(f32[2,3,10,10,130]{4,3,2,1,0:T(8,128)S(1)} %get-tuple-element.718, f32[1,3,9,9,129]{4,3,2,1,0:T(8,128)S(1)} %maximum_bitcast_fusion.6, s32[]{:T(128)} %constant.627.clone.1..sunk, s32[]{:T(128)} %constant.627.clone.1..sunk, s32[]{:T(128)} %constant.642.clone.1..sunk, s32[]{:T(128)} %constant.642.clone.1..sunk, ...) | dynamic-update-slice | bytes 250780 | tf_op jit(solution)/shard_map/while/body/eval_jaxpr/scatter | solution.py:138
  338.2 5.6 %scatter.60 = f32[2,3,10,10,130]{4,3,2,1,0:T(8,128)S(1)} dynamic-update-slice(f32[2,3,10,10,130]{4,3,2,1,0:T(8,128)S(1)} %scatter.59, f32[1,3,9,9,129]{4,3,2,1,0:T(8,128)S(1)} %maximum_bitcast_fusion.7, s32[]{:T(128)} %constant.642.clone.1..sunk, s32[]{:T(128)} %constant.627.clone.1..sunk, s32[]{:T(128)} %constant.627.clone.1..sunk, s32[]{:T(128)} %constant.627.clone.1..sunk, ...) | dynamic-update-slice | bytes 250780 | tf_op jit(solution)/shard_map/while/body/eval_jaxpr/scatter | solution.py:146
  357.6 6.2 %collective-permute-done.2 = f32[3,9,9,1]{3,2,1,0:T(8,128)S(1)} collective-permute-done((f32[3,9,9,1]{3,2,1,0:T(8,128)S(1)}, f32[3,9,9,1]{3,2,1,0:T(8,128)S(1)}, u32[]{:S(2)}, u32[]{:S(2)}) %collective-permute-start.2) | collective-permute-done | bytes 1004 | tf_op jit(solution)/shard_map/while/body/eval_jaxpr/ppermute | solution.py:19
  363.9 13.3 %scatter.59 = f32[2,3,10,10,130]{4,3,2,1,0:T(8,128)S(1)} dynamic-update-slice(f32[2,3,10,10,130]{4,3,2,1,0:T(8,128)S(1)} %get-tuple-element.718, f32[1,3,9,9,129]{4,3,2,1,0:T(8,128)S(1)} %maximum_bitcast_fusion.6, s32[]{:T(128)} %constant.627.clone.1..sunk, s32[]{:T(128)} %constant.627.clone.1..sunk, s32[]{:T(128)} %constant.642.clone.1..sunk, s32[]{:T(128)} %constant.642.clone.1..sunk, ...) | dynamic-update-slice | bytes 250780 | tf_op jit(solution)/shard_map/while/body/eval_jaxpr/scatter | solution.py:138
  390.2 5.6 %scatter.60 = f32[2,3,10,10,130]{4,3,2,1,0:T(8,128)S(1)} dynamic-update-slice(f32[2,3,10,10,130]{4,3,2,1,0:T(8,128)S(1)} %scatter.59, f32[1,3,9,9,129]{4,3,2,1,0:T(8,128)S(1)} %maximum_bitcast_fusion.7, s32[]{:T(128)} %constant.642.clone.1..sunk, s32[]{:T(128)} %constant.627.clone.1..sunk, s32[]{:T(128)} %constant.627.clone.1..sunk, s32[]{:T(128)} %constant.627.clone.1..sunk, ...) | dynamic-update-slice | bytes 250780 | tf_op jit(solution)/shard_map/while/body/eval_jaxpr/scatter | solution.py:146
  430.5 13.3 %scatter.30 = f32[2,3,10,10,130]{4,3,2,1,0:T(8,128)S(1)} dynamic-update-slice(f32[2,3,10,10,130]{4,3,2,1,0:T(8,128)S(1)} %get-tuple-element.360, f32[1,3,9,9,129]{4,3,2,1,0:T(8,128)S(1)} %maximum_bitcast_fusion.3, s32[]{:T(128)} %constant.627.clone.1, s32[]{:T(128)} %constant.627.clone.1, s32[]{:T(128)} %constant.642.clone.1, s32[]{:T(128)} %constant.642.clone.1, s32[]{:T(128)} %constant.642.clone.1) | dynamic-update-slice | bytes 250780 | tf_op jit(solution)/shard_map/scatter | solution.py:138
  (637 shorter events, 256.2 us)
Async XLA Ops:
  3.2 5.4 %collective-permute-start.10 = (f32[8,1,8,128]{3,2,1,0:T(8,128)S(1)}, f32[8,1,8,128]{3,2,1,0:T(8,128)S(1)}, u32[]{:S(2)}, u32[]{:S(2)}) collective-permute-start(f32[8,1,8,128]{3,2,1,0:T(8,128)S(1)} %get-tuple-element.570), channel_id=1, source_target_pairs={{8,0},{16,8},{24,16},{0,24},{9,1},{17,9},{25,17},{1,25},{10,2},{18... | collective-permute-start | bytes 98312 | tf_op jit(solution)/shard_map/ppermute | solution.py:30
  3.2 5.4 %collective-permute-start.9 = (f32[8,1,8,128]{3,2,1,0:T(8,128)S(1)}, f32[8,1,8,128]{3,2,1,0:T(8,128)S(1)}, u32[]{:S(2)}, u32[]{:S(2)}) collective-permute-start(f32[8,1,8,128]{3,2,1,0:T(8,128)S(1)} %get-tuple-element.569), channel_id=1, source_target_pairs={{0,8},{8,16},{16,24},{24,0},{1,9},{9,17},{17,25},{25,1},{2,10},{10... | collective-permute-start | bytes 98312 | tf_op jit(solution)/shard_map/ppermute | solution.py:29
  12.2 4.8 %collective-permute-start.8 = (f32[3,9,9,1]{3,2,1,0:T(8,128)S(1)}, f32[3,9,9,1]{3,2,1,0:T(8,128)S(1)}, u32[]{:S(2)}, u32[]{:S(2)}) collective-permute-start(f32[3,9,9,1]{3,2,1,0:T(8,128)S(1)} %pad_maximum_fusion.19), channel_id=1, source_target_pairs={{1,0},{0,1},{3,2},{2,3},{5,4},{4,5},{7,6},{6,7},{9,8},{8,9},{11,10... | collective-permute-start | bytes 2924 | tf_op jit(solution)/shard_map/ppermute | solution.py:19
  33.9 6.2 %collective-permute-start = (f32[3,1,8,128]{3,2,1,0:T(8,128)S(1)}, f32[3,1,8,128]{3,2,1,0:T(8,128)S(1)}, u32[]{:S(2)}, u32[]{:S(2)}) collective-permute-start(f32[3,1,8,128]{3,2,1,0:T(8,128)S(1)} %slice.3059), channel_id=1, source_target_pairs={{8,0},{16,8},{24,16},{0,24},{9,1},{17,9},{25,17},{1,25},{10,2},{18... | collective-permute-start | bytes 36872 | tf_op jit(solution)/shard_map/while/body/eval_jaxpr/ppermute | solution.py:19
  44.4 6.7 %collective-permute-start.2 = (f32[3,9,9,1]{3,2,1,0:T(8,128)S(1)}, f32[3,9,9,1]{3,2,1,0:T(8,128)S(1)}, u32[]{:S(2)}, u32[]{:S(2)}) collective-permute-start(f32[3,9,9,1]{3,2,1,0:T(8,128)S(1)} %pad_maximum_fusion.39), channel_id=1, source_target_pairs={{1,0},{0,1},{3,2},{2,3},{5,4},{4,5},{7,6},{6,7},{9,8},{8,9},{11,10... | collective-permute-start | bytes 2924 | tf_op jit(solution)/shard_map/while/body/eval_jaxpr/ppermute | solution.py:19
  72.7 4.8 %collective-permute-start.5 = (f32[3,9,9,1]{3,2,1,0:T(8,128)S(1)}, f32[3,9,9,1]{3,2,1,0:T(8,128)S(1)}, u32[]{:S(2)}, u32[]{:S(2)}) collective-permute-start(f32[3,9,9,1]{3,2,1,0:T(8,128)S(1)} %pad_maximum_fusion.41), channel_id=1, source_target_pairs={{1,0},{0,1},{3,2},{2,3},{5,4},{4,5},{7,6},{6,7},{9,8},{8,9},{11,10... | collective-permute-start | bytes 2924 | tf_op jit(solution)/shard_map/while/body/eval_jaxpr/ppermute | solution.py:19
  88.0 5.7 %collective-permute-start = (f32[3,1,8,128]{3,2,1,0:T(8,128)S(1)}, f32[3,1,8,128]{3,2,1,0:T(8,128)S(1)}, u32[]{:S(2)}, u32[]{:S(2)}) collective-permute-start(f32[3,1,8,128]{3,2,1,0:T(8,128)S(1)} %slice.3059), channel_id=1, source_target_pairs={{8,0},{16,8},{24,16},{0,24},{9,1},{17,9},{25,17},{1,25},{10,2},{18... | collective-permute-start | bytes 36872 | tf_op jit(solution)/shard_map/while/body/eval_jaxpr/ppermute | solution.py:19
  96.8 6.6 %collective-permute-start.2 = (f32[3,9,9,1]{3,2,1,0:T(8,128)S(1)}, f32[3,9,9,1]{3,2,1,0:T(8,128)S(1)}, u32[]{:S(2)}, u32[]{:S(2)}) collective-permute-start(f32[3,9,9,1]{3,2,1,0:T(8,128)S(1)} %pad_maximum_fusion.39), channel_id=1, source_target_pairs={{1,0},{0,1},{3,2},{2,3},{5,4},{4,5},{7,6},{6,7},{9,8},{8,9},{11,10... | collective-permute-start | bytes 2924 | tf_op jit(solution)/shard_map/while/body/eval_jaxpr/ppermute | solution.py:19
  140.1 5.8 %collective-permute-start = (f32[3,1,8,128]{3,2,1,0:T(8,128)S(1)}, f32[3,1,8,128]{3,2,1,0:T(8,128)S(1)}, u32[]{:S(2)}, u32[]{:S(2)}) collective-permute-start(f32[3,1,8,128]{3,2,1,0:T(8,128)S(1)} %slice.3059), channel_id=1, source_target_pairs={{8,0},{16,8},{24,16},{0,24},{9,1},{17,9},{25,17},{1,25},{10,2},{18... | collective-permute-start | bytes 36872 | tf_op jit(solution)/shard_map/while/body/eval_jaxpr/ppermute | solution.py:19
  148.9 6.6 %collective-permute-start.2 = (f32[3,9,9,1]{3,2,1,0:T(8,128)S(1)}, f32[3,9,9,1]{3,2,1,0:T(8,128)S(1)}, u32[]{:S(2)}, u32[]{:S(2)}) collective-permute-start(f32[3,9,9,1]{3,2,1,0:T(8,128)S(1)} %pad_maximum_fusion.39), channel_id=1, source_target_pairs={{1,0},{0,1},{3,2},{2,3},{5,4},{4,5},{7,6},{6,7},{9,8},{8,9},{11,10... | collective-permute-start | bytes 2924 | tf_op jit(solution)/shard_map/while/body/eval_jaxpr/ppermute | solution.py:19
  192.2 5.8 %collective-permute-start = (f32[3,1,8,128]{3,2,1,0:T(8,128)S(1)}, f32[3,1,8,128]{3,2,1,0:T(8,128)S(1)}, u32[]{:S(2)}, u32[]{:S(2)}) collective-permute-start(f32[3,1,8,128]{3,2,1,0:T(8,128)S(1)} %slice.3059), channel_id=1, source_target_pairs={{8,0},{16,8},{24,16},{0,24},{9,1},{17,9},{25,17},{1,25},{10,2},{18... | collective-permute-start | bytes 36872 | tf_op jit(solution)/shard_map/while/body/eval_jaxpr/ppermute | solution.py:19
  200.9 6.6 %collective-permute-start.2 = (f32[3,9,9,1]{3,2,1,0:T(8,128)S(1)}, f32[3,9,9,1]{3,2,1,0:T(8,128)S(1)}, u32[]{:S(2)}, u32[]{:S(2)}) collective-permute-start(f32[3,9,9,1]{3,2,1,0:T(8,128)S(1)} %pad_maximum_fusion.39), channel_id=1, source_target_pairs={{1,0},{0,1},{3,2},{2,3},{5,4},{4,5},{7,6},{6,7},{9,8},{8,9},{11,10... | collective-permute-start | bytes 2924 | tf_op jit(solution)/shard_map/while/body/eval_jaxpr/ppermute | solution.py:19
  244.3 5.8 %collective-permute-start = (f32[3,1,8,128]{3,2,1,0:T(8,128)S(1)}, f32[3,1,8,128]{3,2,1,0:T(8,128)S(1)}, u32[]{:S(2)}, u32[]{:S(2)}) collective-permute-start(f32[3,1,8,128]{3,2,1,0:T(8,128)S(1)} %slice.3059), channel_id=1, source_target_pairs={{8,0},{16,8},{24,16},{0,24},{9,1},{17,9},{25,17},{1,25},{10,2},{18... | collective-permute-start | bytes 36872 | tf_op jit(solution)/shard_map/while/body/eval_jaxpr/ppermute | solution.py:19
  253.1 6.7 %collective-permute-start.2 = (f32[3,9,9,1]{3,2,1,0:T(8,128)S(1)}, f32[3,9,9,1]{3,2,1,0:T(8,128)S(1)}, u32[]{:S(2)}, u32[]{:S(2)}) collective-permute-start(f32[3,9,9,1]{3,2,1,0:T(8,128)S(1)} %pad_maximum_fusion.39), channel_id=1, source_target_pairs={{1,0},{0,1},{3,2},{2,3},{5,4},{4,5},{7,6},{6,7},{9,8},{8,9},{11,10... | collective-permute-start | bytes 2924 | tf_op jit(solution)/shard_map/while/body/eval_jaxpr/ppermute | solution.py:19
  296.3 5.8 %collective-permute-start = (f32[3,1,8,128]{3,2,1,0:T(8,128)S(1)}, f32[3,1,8,128]{3,2,1,0:T(8,128)S(1)}, u32[]{:S(2)}, u32[]{:S(2)}) collective-permute-start(f32[3,1,8,128]{3,2,1,0:T(8,128)S(1)} %slice.3059), channel_id=1, source_target_pairs={{8,0},{16,8},{24,16},{0,24},{9,1},{17,9},{25,17},{1,25},{10,2},{18... | collective-permute-start | bytes 36872 | tf_op jit(solution)/shard_map/while/body/eval_jaxpr/ppermute | solution.py:19
  305.0 6.5 %collective-permute-start.2 = (f32[3,9,9,1]{3,2,1,0:T(8,128)S(1)}, f32[3,9,9,1]{3,2,1,0:T(8,128)S(1)}, u32[]{:S(2)}, u32[]{:S(2)}) collective-permute-start(f32[3,9,9,1]{3,2,1,0:T(8,128)S(1)} %pad_maximum_fusion.39), channel_id=1, source_target_pairs={{1,0},{0,1},{3,2},{2,3},{5,4},{4,5},{7,6},{6,7},{9,8},{8,9},{11,10... | collective-permute-start | bytes 2924 | tf_op jit(solution)/shard_map/while/body/eval_jaxpr/ppermute | solution.py:19
  348.4 5.8 %collective-permute-start = (f32[3,1,8,128]{3,2,1,0:T(8,128)S(1)}, f32[3,1,8,128]{3,2,1,0:T(8,128)S(1)}, u32[]{:S(2)}, u32[]{:S(2)}) collective-permute-start(f32[3,1,8,128]{3,2,1,0:T(8,128)S(1)} %slice.3059), channel_id=1, source_target_pairs={{8,0},{16,8},{24,16},{0,24},{9,1},{17,9},{25,17},{1,25},{10,2},{18... | collective-permute-start | bytes 36872 | tf_op jit(solution)/shard_map/while/body/eval_jaxpr/ppermute | solution.py:19
  357.2 6.7 %collective-permute-start.2 = (f32[3,9,9,1]{3,2,1,0:T(8,128)S(1)}, f32[3,9,9,1]{3,2,1,0:T(8,128)S(1)}, u32[]{:S(2)}, u32[]{:S(2)}) collective-permute-start(f32[3,9,9,1]{3,2,1,0:T(8,128)S(1)} %pad_maximum_fusion.39), channel_id=1, source_target_pairs={{1,0},{0,1},{3,2},{2,3},{5,4},{4,5},{7,6},{6,7},{9,8},{8,9},{11,10... | collective-permute-start | bytes 2924 | tf_op jit(solution)/shard_map/while/body/eval_jaxpr/ppermute | solution.py:19
  385.1 4.8 %collective-permute-start.5 = (f32[3,9,9,1]{3,2,1,0:T(8,128)S(1)}, f32[3,9,9,1]{3,2,1,0:T(8,128)S(1)}, u32[]{:S(2)}, u32[]{:S(2)}) collective-permute-start(f32[3,9,9,1]{3,2,1,0:T(8,128)S(1)} %pad_maximum_fusion.41), channel_id=1, source_target_pairs={{1,0},{0,1},{3,2},{2,3},{5,4},{4,5},{7,6},{6,7},{9,8},{8,9},{11,10... | collective-permute-start | bytes 2924 | tf_op jit(solution)/shard_map/while/body/eval_jaxpr/ppermute | solution.py:19
  402.6 5.2 %collective-permute-start.15 = (f32[2,1,8,128]{3,2,1,0:T(8,128)S(1)}, f32[2,1,8,128]{3,2,1,0:T(8,128)S(1)}, u32[]{:S(2)}, u32[]{:S(2)}) collective-permute-start(f32[2,1,8,128]{3,2,1,0:T(8,128)S(1)} %get-tuple-element.575), channel_id=1, source_target_pairs={{0,8},{8,16},{16,24},{24,0},{1,9},{9,17},{17,25},{25,1},{2,10},{10... | collective-permute-start | bytes 24584 | tf_op jit(solution)/shard_map/ppermute | solution.py:29
  410.1 6.9 %collective-permute-start.17 = (f32[2,10,1,128]{3,2,1,0:T(1,128)S(1)}, f32[2,10,1,128]{3,2,1,0:T(1,128)S(1)}, u32[]{:S(2)}, u32[]{:S(2)}) collective-permute-start(f32[2,10,1,128]{3,2,1,0:T(1,128)S(1)} %get-tuple-element.573), channel_id=1, source_target_pairs={{0,2},{2,4},{4,6},{6,0},{1,3},{3,5},{5,7},{7,1},{8,10},{10,12},{12... | collective-permute-start | bytes 30728 | tf_op jit(solution)/shard_map/ppermute | solution.py:29
  410.4 6.6 %collective-permute-start.18 = (f32[2,10,1,128]{3,2,1,0:T(1,128)S(1)}, f32[2,10,1,128]{3,2,1,0:T(1,128)S(1)}, u32[]{:S(2)}, u32[]{:S(2)}) collective-permute-start(f32[2,10,1,128]{3,2,1,0:T(1,128)S(1)} %get-tuple-element.574), channel_id=1, source_target_pairs={{2,0},{4,2},{6,4},{0,6},{3,1},{5,3},{7,5},{1,7},{10,8},{12,10},{14... | collective-permute-start | bytes 30728 | tf_op jit(solution)/shard_map/ppermute | solution.py:30
  417.4 7.9 %collective-permute-start.20 = (f32[2,10,10,1]{3,2,1,0:T(8,128)S(1)}, f32[2,10,10,1]{3,2,1,0:T(8,128)S(1)}, u32[]{:S(2)}, u32[]{:S(2)}) collective-permute-start(f32[2,10,10,1]{3,2,1,0:T(8,128)S(1)} %get-tuple-element.572), channel_id=1, source_target_pairs={{1,0},{0,1},{3,2},{2,3},{5,4},{4,5},{7,6},{6,7},{9,8},{8,9},{11,10... | collective-permute-start | bytes 2408 | tf_op jit(solution)/shard_map/ppermute | solution.py:30
  419.3 6.3 %collective-permute-start.22 = (f32[3,9,1,128]{3,2,1,0:T(1,128)S(1)}, f32[3,9,1,128]{3,2,1,0:T(1,128)S(1)}, u32[]{:S(2)}, u32[]{:S(2)}) collective-permute-start(f32[3,9,1,128]{3,2,1,0:T(1,128)S(1)} %pad_maximum_fusion.29), channel_id=1, source_target_pairs={{2,0},{4,2},{6,4},{0,6},{3,1},{5,3},{7,5},{1,7},{10,8},{12,10},{14... | collective-permute-start | bytes 41480 | tf_op jit(solution)/shard_map/ppermute | solution.py:19
  (134 other events, 883.5 us)
where the time goes:
time: 459 us; the launch traced here: 454 us
  local copies, waits for them, and re-layouts  189 us (41%)
  waiting for transfers between devices  150 us (33%)
  starting transfers between devices  80.7 us (18%)
  other arithmetic  29.2 us (6%)
    ppermute x48, waiting for transfers between devices, shifted(): return lax.ppermute(block, axis, route)  140 us
    scatter x8, local copies, waits for them, and re-layouts, lower_update(): ghosts = ghosts.at[0, :, 1:, 1:, 1:].set(send_upper(turned))  107 us
    ppermute x48, starting transfers between devices, shifted(): return lax.ppermute(block, axis, route)  63.7 us
    scatter x7, local copies, waits for them, and re-layouts, upper_update(): ghosts = ghosts.at[1, :, :-1, :-1, :-1].set(send_lower(turned))  38.9 us
    slice x45, local copies, waits for them, and re-layouts, window_of(): return lax.slice(values, starts, limits)  24.1 us
    ppermute x6, starting transfers between devices, padded_2(): before = lax.ppermute(last, axis, up)  9.35 us
  transfers between devices with their start and end apart: 60, of which 52 were waited for; matrix products, arithmetic and copies ran while one was open for 2% of the time, Pallas kernels for 0%

commit v1 on v0

v1 whole, which is shorter than its diff:
```python
import functools
import itertools

import jax
import jax.numpy as jnp
from jax import lax
from jax.experimental import pallas as pl
from jax.experimental.pallas import tpu as pltpu
from jax.sharding import PartitionSpec as P

step_time = 0.6
exchange_scale = 0.35
exchange_decay = 4.0
pair_scale = 0.5
pair_decay = 6.0
density_decay = 3.0
bond_length = 0.8660254037844386
corner_offsets = list(itertools.product((0, 1), repeat=3))
axes = ("gx", "gy", "gz")
MESH = pl.DeviceIdType.MESH

FIELDS = 14
STRIPS = 2


def working(rows, lanes):
    row = lax.broadcasted_iota(jnp.int32, (rows, lanes), 0)
    first, last = row % 4 == 0, row % 4 == 3

    def turn(v, n):
        return pltpu.roll(v, n % rows, 0)

    def below(pair, tile):
        a, b = pair
        if tile == 0:
            return jnp.where(first, turn(b, 5), turn(a, 1))
        return jnp.where(first, turn(a, 1), turn(b, 1))

    def above(pair, tile):
        a, b = pair
        if tile == 0:
            return jnp.where(last, turn(b, -1), turn(a, -1))
        return jnp.where(last, turn(a, 3), turn(b, -1))

    def z_below(v):
        return pltpu.roll(v, 1, 1)

    def z_above(v):
        return pltpu.roll(v, lanes - 1, 1)

    return below, above, z_below, z_above


def kernel(sizes, spin, disp, occ, field, out_s, out_f, E, PZ, RZ, SY, RY, W, WZ, J, J1, P3, RI, FS, FZ, ACC,
           send_sem, recv_sem):
    nx, ny, nz = sizes
    me = {a: lax.axis_index(a) for a in axes}
    count = dict(zip(axes, sizes))

    def peer(axis, step):
        n = count[axis]
        return {axis: lax.rem(me[axis] + (n + step), n)}

    peers = []
    for axis in axes:
        peers.append(peer(axis, 1))
        if count[axis] > 2:
            peers.append(peer(axis, -1))
    barrier = pltpu.get_barrier_semaphore()
    for p in peers:
        pl.semaphore_signal(barrier, inc=1, device_id=p, device_id_type=MESH)

    lane = lax.broadcasted_iota(jnp.int32, (8, 128), 1)
    row = lax.broadcasted_iota(jnp.int32, (8, 128), 0)
    upper = row < 4

    def swap(v):
        return pltpu.roll(v, 4, 0)

    def load_own(x, _):
        packed = [jnp.zeros((8, 128), jnp.float32)] * STRIPS
        for f in range(FIELDS):
            if f < 6:
                v = spin[f // 3, f % 3, x]
            elif f < 12:
                v = disp[(f - 6) // 3, f % 3, x]
            else:
                v = occ[f - 12, x].astype(jnp.float32)
            E[f, x, 0] = v
            g = f % 7
            moved = pltpu.roll(v, 8 + 16 * g, 1)
            packed[f // 7] = jnp.where(lane // 16 == g, moved, packed[f // 7])
        for s in range(STRIPS):
            PZ[s, x] = packed[s]
        return 0

    lax.fori_loop(0, 8, load_own, 0)

    def pack_rows(f, _):
        for x in range(4):
            a, b = E[f, x, 0], E[f, x + 4, 0]
            SY[0, f, x] = jnp.where(upper, a, swap(b))
            SY[1, f, x] = jnp.where(upper, swap(a), b)
        return 0

    lax.fori_loop(0, FIELDS, pack_rows, 0)
    pl.semaphore_wait(barrier, len(peers))

    def send(i, src, dst, to):
        c = pltpu.make_async_remote_copy(
            src_ref=src, dst_ref=dst, send_sem=send_sem.at[i], recv_sem=recv_sem.at[i],
            device_id=to, device_id_type=MESH)
        c.start()
        return c

    def exchange_x(i, lo, n, part, low, high):
        return [
            send(i, E.at[pl.ds(lo, n), pl.ds(0, low), part], E.at[pl.ds(lo, n), pl.ds(8, low), part], peer("gx", -1)),
            send(i + 1, E.at[pl.ds(lo, n), pl.ds(8 - high, high), part],
                 E.at[pl.ds(lo, n), pl.ds(16 - high, high), part], peer("gx", 1)),
        ]

    def exchange_y(i, lo, n):
        return [
            send(i, SY.at[0, pl.ds(lo, n)], RY.at[0, pl.ds(lo, n)], peer("gy", -1)),
            send(i + 1, SY.at[1, pl.ds(lo, n)], RY.at[1, pl.ds(lo, n)], peer("gy", 1)),
        ]

    zs = [send(0, PZ, RZ.at[0], peer("gz", -1))]
    if nz > 2:
        zs.append(send(1, PZ, RZ.at[1], peer("gz", 1)))
    ys = exchange_y(2, 0, FIELDS)
    xs = exchange_x(4, 0, FIELDS, 0, 4, 4)
    for c in zs:
        c.wait()
    for s in range(STRIPS):
        for x in range(8):
            v = RZ[0, s, x]
            if nz > 2:
                v = jnp.where(lane % 16 < 8, RZ[1, s, x], v)
            E[FIELDS + s, x, 0] = v
    lax.fori_loop(FIELDS, FIELDS + STRIPS, pack_rows, 0)
    ys2 = exchange_y(6, FIELDS, STRIPS)
    xs2 = exchange_x(8, FIELDS, STRIPS, 0, 4, 4)

    def unpack_rows(f, _):
        for x in range(4):
            lo, hi = RY[0, f, x], RY[1, f, x]
            E[f, x, 1] = jnp.where(upper, lo, swap(hi))
            E[f, x + 4, 1] = jnp.where(upper, swap(lo), hi)
        return 0

    for c in ys:
        c.wait()
    lax.fori_loop(0, FIELDS, unpack_rows, 0)
    xs3 = exchange_x(10, 0, FIELDS, 1, 2, 2)
    for c in ys2:
        c.wait()
    lax.fori_loop(FIELDS, FIELDS + STRIPS, unpack_rows, 0)
    xs4 = exchange_x(12, FIELDS, STRIPS, 1, 2, 2)
    for c in xs + xs2 + xs3 + xs4:
        c.wait()

    below, above, z_below, z_above = working(8, 256)

    def build(x, _):
        def tiles(f):
            t, g = E[f, x, 0], swap(E[f, x, 1])
            return jnp.where(upper, t, g), jnp.where(upper, g, t)

        strips = [tiles(FIELDS + s) for s in range(STRIPS)]
        for f in range(FIELDS):
            pair = tiles(f)
            for t in range(2):
                halo = pltpu.roll(strips[f // 7][t], 128 - 16 * (f % 7) - 8, 1)
                v = jnp.concatenate([pair[t], halo], axis=1)
                W[f, x, t] = v
                if f < 3:
                    WZ[f, x, t] = z_above(v)
                elif f < 6 or f in (9, 10, 11, 13):
                    WZ[f, x, t] = z_below(v)
        return 0

    lax.fori_loop(0, 16, build, 0)

    def before(x):
        return lax.rem(x + 15, 16)

    def after(x):
        return lax.rem(x + 1, 16)

    def pair_of(ref, f, x):
        return ref[f, x, 0], ref[f, x, 1]

    def partner(f, planes, o, tile):
        ref = WZ if o[2] else W
        if o[1]:
            return below(pair_of(ref, f, planes[o[0]]), tile)
        return ref[f, planes[o[0]], tile]

    def bonds(x, _):
        planes = (x, before(x))
        for t in range(2):
            own = [W[6 + k, x, t] for k in range(3)]
            here = W[12, x, t]
            for i, o in enumerate(corner_offsets):
                d = [(0.5 - o[k]) + (partner(9 + k, planes, o, t) - own[k]) for k in range(3)]
                w = here * partner(13, planes, o, t)
                r2 = d[0] * d[0] + d[1] * d[1] + d[2] * d[2]
                inverse = lax.rsqrt(r2)
                stretch = r2 * inverse - bond_length
                J[i, x, t] = w * exchange_scale * jnp.exp(-exchange_decay * stretch)
                P3[i, x, t] = w * jnp.exp(-density_decay * stretch)
                RI[i, x, t] = inverse
        return 0

    lax.fori_loop(0, 16, bonds, 0)

    def upper_bonds(x, _):
        planes = (x, after(x))
        for i, o in enumerate(corner_offsets):
            pair = pair_of(J, i, planes[o[0]])
            if o[2]:
                pair = [z_above(v) for v in pair]
            for t in range(2):
                J1[i, x, t] = above(pair, t) if o[1] else pair[t]
        return 0

    lax.fori_loop(0, 16, upper_bonds, 0)

    def update(u):
        sector = u if u < 8 else 14 - u
        sub, quarter = sector % 2, sector // 2
        half, tile = quarter % 2, quarter // 2
        scale = 0.5 * (step_time if u == 7 else 0.5 * step_time)
        source = 3 if sub == 0 else 0
        target = 3 * sub
        coupling = J if sub == 0 else J1

        def plane(x, _):
            planes = (x, before(x) if sub == 0 else after(x))
            h = [field[k] for k in range(3)]
            for k in range(3):
                total = None
                for ox in range(2):
                    for oz in range(2):
                        ref = WZ if oz else W
                        pair = pair_of(ref, source + k, planes[ox])
                        for oy in range(2):
                            i = 4 * ox + 2 * oy + oz
                            v = pair[tile] if oy == 0 else (below if sub == 0 else above)(pair, tile)
                            term = coupling[i, x, tile] * v
                            total = term if total is None else total + term
                h[k] = (h[k] + total) * scale
            s = [W[target + k, x, tile] for k in range(3)]

            def cross(a, b):
                return [a[1] * b[2] - a[2] * b[1], a[2] * b[0] - a[0] * b[2], a[0] * b[1] - a[1] * b[0]]

            once = cross(h, s)
            twice = cross(h, once)
            factor = 2.0 / (1.0 + (h[0] * h[0] + h[1] * h[1] + h[2] * h[2]))
            for k in range(3):
                v = s[k] + factor * (once[k] + twice[k])
                W[target + k, x, tile] = v
                WZ[target + k, x, tile] = z_above(v) if sub == 0 else z_below(v)
            return 0

        def pairs(m, _):
            base = 4 * half + 8 * m
            for n in range(4):
                plane(base + n, 0)
            return 0

        lax.fori_loop(0, 2, pairs, 0)

    for u in range(15):
        update(u)

    def slope(rho):
        return -0.5 * lax.rsqrt(1.0 + rho)

    def slopes(n, _):
        x = lax.rem(n + 15, 16)
        planes = (x, after(x))
        for t in range(2):
            FS[0, x, t] = slope(functools.reduce(jnp.add, [P3[i, x, t] for i in range(8)]))
        rows = []
        for oy in range(2):
            total = []
            for t in range(2):
                flat = P3[2 * oy, planes[0], t] + P3[4 + 2 * oy, planes[1], t]
                high = P3[2 * oy + 1, planes[0], t] + P3[5 + 2 * oy, planes[1], t]
                total.append(flat + z_above(high))
            rows.append(total)
        for t in range(2):
            v = slope(rows[0][t] + above(rows[1], t))
            FS[1, x, t] = v
            FZ[x, t] = z_below(v)
        return 0

    lax.fori_loop(0, 10, slopes, 0)

    def slope_partner(planes, o, tile):
        x = planes[o[0]]
        pair = (FZ[x, 0], FZ[x, 1]) if o[2] else (FS[1, x, 0], FS[1, x, 1])
        return below(pair, tile) if o[1] else pair[tile]

    def forces(x, _):
        planes = (x, before(x))
        sums = [[None] * 2 for _ in range(3)]
        parts = {}
        for t in range(2):
            own = [W[6 + k, x, t] for k in range(3)]
            spins = [W[k, x, t] for k in range(3)]
            mine = FS[0, x, t]
            for i, o in enumerate(corner_offsets):
                d = [(0.5 - o[k]) + (partner(9 + k, planes, o, t) - own[k]) for k in range(3)]
                align = functools.reduce(jnp.add, [spins[k] * partner(3 + k, planes, o, t) for k in range(3)])
                p = P3[i, x, t]
                g = (-pair_decay * pair_scale * (p * p) - density_decay * p * (mine + slope_partner(planes, o, t))
                     + exchange_decay * J[i, x, t] * align) * RI[i, x, t]
                for k in range(3):
                    v = g * d[k]
                    parts[i, t, k] = v
                    sums[k][t] = v if sums[k][t] is None else sums[k][t] + v
        for k in range(3):
            for t in range(2):
                ACC[k, x, t] = sums[k][t]
            for ox in range(2):
                rows = [[parts[4 * ox + 2 * oy, t, k] + z_above(parts[4 * ox + 2 * oy + 1, t, k]) for t in range(2)]
                        for oy in range(2)]
                for t in range(2):
                    v = rows[0][t] + above(rows[1], t)
                    if ox == 0:
                        ACC[3 + k, x, t] = -v
                    else:
                        ACC[3 + k, planes[1], t] = ACC[3 + k, planes[1], t] - v
        return 0

    lax.fori_loop(0, 9, forces, 0)

    def write(x, _):
        for f in range(6):
            for ref, out in ((W, out_s), (ACC, out_f)):
                a, b = ref[f, x, 0], ref[f, x, 1]
                out[f // 3, f % 3, x] = jnp.where(upper, a[:, :128], b[:, :128])
        return 0

    lax.fori_loop(0, 8, write, 0)


def on_device(sizes, spin_vectors, displacement, occupied, applied_field):
    vmem = pl.BlockSpec(memory_space=pltpu.VMEM)
    smem = pl.BlockSpec(memory_space=pltpu.SMEM)
    shape = jax.ShapeDtypeStruct(spin_vectors.shape, jnp.float32)

    def buffer(*lead):
        return pltpu.VMEM(lead + (8, 128), jnp.float32)

    def wide(*lead):
        return pltpu.VMEM(lead + (16, 2, 8, 256), jnp.float32)

    return pl.pallas_call(
        functools.partial(kernel, sizes),
        out_shape=(shape, shape),
        in_specs=[vmem, vmem, vmem, smem],
        out_specs=(vmem, vmem),
        scratch_shapes=[
            buffer(FIELDS + STRIPS, 16, 2),
            buffer(STRIPS, 8),
            buffer(2, STRIPS, 8),
            buffer(2, FIELDS + STRIPS, 4),
            buffer(2, FIELDS + STRIPS, 4),
            wide(FIELDS), wide(FIELDS), wide(8), wide(8), wide(8), wide(8), wide(2), wide(), wide(6),
            pltpu.SemaphoreType.DMA((14,)),
            pltpu.SemaphoreType.DMA((14,)),
        ],
        compiler_params=pltpu.CompilerParams(
            collective_id=0, has_side_effects=True, vmem_limit_bytes=60 * 1024 * 1024),
    )(spin_vectors, displacement, occupied, applied_field)


def solution(mesh):
    sizes = tuple(mesh.shape[a] for a in axes)
    block = P(None, None, "gx", "gy", "gz")
    return jax.shard_map(
        functools.partial(on_device, sizes),
        mesh=mesh,
        in_specs=(block, block, P(None, "gx", "gy", "gz"), P()),
        out_specs=(block, block),
        check_vma=False,
    )
```

time: 459 us -> 48.7 us (0.11); the launches traced: 454 us -> 48.6 us
  local copies, waits for them, and re-layouts: 189 us -> 2.34 us
  waiting for transfers between devices: 150 us -> 0 us
  starting transfers between devices: 80.7 us -> 0 us
  Pallas kernels: 0 us -> 45.6 us
  other arithmetic: 29.2 us -> 0 us
    ppermute x60 -> x0, waiting for transfers between devices: 150 us -> none  [the longest x48 140 us: shifted(): return lax.ppermute(block, axis, route)]
    scatter x16 -> x0, local copies, waits for them, and re-layouts: 146 us -> none  [the longest x8 107 us: lower_update(): ghosts = ghosts.at[0, :, 1:, 1:, 1:].set(send_upper(turned))]
    ppermute x60 -> x0, starting transfers between devices: 80.7 us -> none  [the longest x48 63.7 us: shifted(): return lax.ppermute(block, axis, route)]
    pallas_call x0 -> x1, Pallas kernels: none -> 45.6 us  [on_device(): pl.pallas_call(functools.partial(kernel, sizes), out_shape=(shape, shape)...]
    slice x66 -> x0, local copies, waits for them, and re-layouts: 25.7 us -> none  [the longest x45 24.1 us: window_of(): return lax.slice(values, starts, limits)]
    reduce_sum x23 -> x0, other arithmetic: 10.1 us -> none  [the longest x15 9.05 us: rotate(): factor = 2.0 / (1.0 + jnp.sum(rotation * rotation, axis=0))]
    squeeze x27 -> x0, local copies, waits for them, and re-layouts: 7.38 us -> none  [the longest x8 6.65 us: first_field(): bond_term = window_of(coupling[corner], lowest, (0, 0, 0), 0, counts)]
    another operation x20 -> x0, other arithmetic: 5.08 us -> none
  transfers between devices with their start and end apart: 60 -> 0, of which waited for: 52 -> 0; matrix products, arithmetic and copies ran while one was open for 2% -> 0% of each run, Pallas kernels for 0% -> 0%
where the time goes in v1:
time: 48.7 us; the launch traced here: 48.6 us
  Pallas kernels  45.6 us (94%)
  local copies, waits for them, and re-layouts  2.34 us (5%)
  between operations  0.65 us (1%)
    pallas_call x1, Pallas kernels, on_device(): pl.pallas_call(functools.partial(kernel, sizes), out_shape=(shape, shape)...  45.6 us
    unnamed x4, local copies, waits for them, and re-layouts  2.34 us

profile of v1, /device:TPU:1, one launch (start us, length us, event | category | flops | bytes accessed | tf_op | source)
XLA Modules:
  0.0 48.6 jit_solution(16426842765204064620)
XLA Ops:
  0.6 45.6 %shard_map.59 = (f32[2,3,8,8,128]{4,3,2,1,0:T(8,128)}, f32[2,3,8,8,128]{4,3,2,1,0:T(8,128)}) custom-call(f32[2,3,8,8,128]{4,3,2,1,0:T(8,128)} %spin.1, f32[2,3,8,8,128]{4,3,2,1,0:T(8,128)} %disp.1, s32[2,8,8,128]{3,2,1,0:T(8,128)} %occ.1, f32[3]{0:T(128)} %field.1), custom_call_target="tpu_custom_call" | custom-call | tf_op jit(solution)/shard_map/pallas_call | solution.py:364
  46.2 0.0 copy-start
  46.2 1.7 %copy.8 = f32[2,3,8,8,128]{4,3,2,1,0:T(8,128)} copy(f32[2,3,8,8,128]{4,3,2,1,0:T(8,128)} %get-tuple-element.4) | data formatting | bytes 393216
  47.9 0.0 copy-done
  47.9 0.7 %copy.9 = f32[2,3,8,8,128]{4,3,2,1,0:T(8,128)} copy(f32[2,3,8,8,128]{4,3,2,1,0:T(8,128)S(1)} %copy-done) | data formatting | bytes 393216
Async XLA Ops:
  46.2 1.7 %copy-start = (f32[2,3,8,8,128]{4,3,2,1,0:T(8,128)S(1)}, f32[2,3,8,8,128]{4,3,2,1,0:T(8,128)}, u32[]{:S(2)}) copy-start(f32[2,3,8,8,128]{4,3,2,1,0:T(8,128)} %get-tuple-element.5) | copy-start | bytes 589828

commit v2 on v1

v2 whole, which is shorter than its diff:
```python
import functools
import itertools

import jax
import jax.numpy as jnp
from jax import lax
from jax.experimental import pallas as pl
from jax.experimental.pallas import tpu as pltpu
from jax.sharding import PartitionSpec as P

step_time = 0.6
exchange_scale = 0.35
exchange_decay = 4.0
pair_scale = 0.5
pair_decay = 6.0
density_decay = 3.0
bond_length = 0.8660254037844386
corner_offsets = list(itertools.product((0, 1), repeat=3))
axes = ("gx", "gy", "gz")
MESH = pl.DeviceIdType.MESH

FIELDS = 7
TO_BELOW = tuple(
    [(i // 4, i, 0, 2, 2 * (i % 4)) for i in range(8)] + [(2, 2 + i, 2, 2, 2 * i) for i in range(4)])
TO_ABOVE_0 = tuple([(0, i, 7, 1, i) for i in range(8)] + [(1, 2 + i, 5, 2, 2 * i) for i in range(4)])
TO_ABOVE_1 = tuple(
    [(i // 4, i, 6, 2, 2 * (i % 4)) for i in range(8)] + [(2, 2 + i, 4, 2, 2 * i) for i in range(4)])


@functools.cache
def turned_planes():
    need = {(0, x, y) for x in range(9) for y in range(9)} | {(1, x, y) for x in range(-1, 8) for y in range(-1, 8)}
    need |= {(b, x, y) for b in (0, 1) for x in range(8) for y in range(8)}
    planes = {}
    for u in reversed(range(15)):
        sector = u if u < 8 else 14 - u
        sub, quarter = sector % 2, sector // 2
        turned = [k for k in need if k[0] == sub and k[1] // 4 % 2 + 2 * (k[2] // 4 % 2) == quarter]
        planes[u] = sorted({k[1] for k in turned})
        for _, x, y in turned:
            for a, b, _ in corner_offsets:
                need.add((1, x - a, y - b) if sub == 0 else (0, x + a, y + b))
    return planes


def working(rows, lanes):
    row = lax.broadcasted_iota(jnp.int32, (rows, lanes), 0)
    first, last = row % 4 == 0, row % 4 == 3

    def turn(v, n):
        return pltpu.roll(v, n % rows, 0)

    def below(pair, tile):
        a, b = pair
        if tile == 0:
            return jnp.where(first, turn(b, 5), turn(a, 1))
        return jnp.where(first, turn(a, 1), turn(b, 1))

    def above(pair, tile):
        a, b = pair
        if tile == 0:
            return jnp.where(last, turn(b, -1), turn(a, -1))
        return jnp.where(last, turn(a, 3), turn(b, -1))

    def z_below(v):
        return pltpu.roll(v, 1, 1)

    def z_above(v):
        return pltpu.roll(v, lanes - 1, 1)

    return below, above, z_below, z_above


def kernel(sizes, spin, disp, occ, field, out_s, out_f, E, PZ, RZ, SU, RU, SD, RD, SX, RX, SC, RC, W, WZ, J, J1, P3, RI, FS, FZ, ACC,
           send_sem, recv_sem):
    nx, ny, nz = sizes
    me = {a: lax.axis_index(a) for a in axes}
    count = dict(zip(axes, sizes))

    def peer(axis, step):
        n = count[axis]
        return {axis: lax.rem(me[axis] + (n + step), n)}

    peers = []
    for axis in axes:
        peers.append(peer(axis, 1))
        if count[axis] > 2:
            peers.append(peer(axis, -1))
    barrier = pltpu.get_barrier_semaphore()
    for p in peers:
        pl.semaphore_signal(barrier, inc=1, device_id=p, device_id_type=MESH)

    lane = lax.broadcasted_iota(jnp.int32, (8, 128), 1)
    row = lax.broadcasted_iota(jnp.int32, (8, 128), 0)
    upper = row < 4

    def swap(v):
        return pltpu.roll(v, 4, 0)

    def load_own(x, _):
        for s in range(2):
            packed = jnp.zeros((8, 128), jnp.float32)
            for f in range(FIELDS):
                if f < 3:
                    v = spin[s, f, x]
                elif f < 6:
                    v = disp[s, f - 3, x]
                else:
                    v = occ[s, x].astype(jnp.float32)
                E[s, f, x, 0] = v
                packed = jnp.where(lane // 16 == f, pltpu.roll(v, 8 + 16 * f, 1), packed)
            PZ[s, x] = packed
        return 0

    lax.fori_loop(0, 8, load_own, 0)
    inner = (row >= 2) & (row < 6)

    def routes(s):
        return ((SU, RU, (0, 2)[s], (TO_ABOVE_0, TO_ABOVE_1)[s]), (SD, RD, 3 * s, TO_BELOW))

    def pack_rows(f, _):
        for s in range(2):
            own = [E[s, f, x, 0] for x in range(8)]
            for out, _unused, first, pieces in routes(s):
                tiles = {}
                for tile, x, low, n, to in pieces:
                    v = pltpu.roll(own[x], (to - low) % 8, 0)
                    tiles[tile] = jnp.where(row < to, tiles[tile], v) if to else v
                for tile, v in tiles.items():
                    out[f, first + tile] = v
            SX[0, s, f] = jnp.where(inner, own[2], swap(own[3]))
            SX[1, s, f] = jnp.where(inner, own[4], swap(own[5]))
        return 0

    def unpack_rows(f, _):
        for s in range(2):
            rows = [jnp.zeros((8, 128), jnp.float32)] * 8
            for _unused, arrived, first, pieces in routes(s):
                for tile, x, low, n, to in pieces:
                    v = pltpu.roll(arrived[f, first + tile], (low - to) % 8, 0)
                    rows[x] = jnp.where((row >= low) & (row < low + n), v, rows[x])
            for x in range(8):
                E[s, f, x, 1] = rows[x]
            SC[0, s, f] = jnp.where(inner, swap(rows[1]), rows[0])
            SC[1, s, f] = jnp.where(inner, swap(rows[7]), rows[6])
        return 0

    lax.fori_loop(0, FIELDS, pack_rows, 0)
    pl.semaphore_wait(barrier, len(peers))

    def send(i, src, dst, to):
        c = pltpu.make_async_remote_copy(
            src_ref=src, dst_ref=dst, send_sem=send_sem.at[i], recv_sem=recv_sem.at[i],
            device_id=to, device_id_type=MESH)
        c.start()
        return c

    def exchange_y(i, lo, n):
        return [
            send(i, SD.at[pl.ds(lo, n)], RD.at[pl.ds(lo, n)], peer("gy", -1)),
            send(i + 1, SU.at[pl.ds(lo, n)], RU.at[pl.ds(lo, n)], peer("gy", 1)),
        ]

    def exchange_x(i, lo, n):
        def plane(x):
            return E.at[:, pl.ds(lo, n), pl.ds(x, 2), 0]

        return [
            send(i, plane(0), plane(8), peer("gx", -1)),
            send(i + 1, plane(6), plane(14), peer("gx", 1)),
            send(i + 2, SX.at[0, :, pl.ds(lo, n)], RX.at[0, :, pl.ds(lo, n)], peer("gx", -1)),
            send(i + 3, SX.at[1, :, pl.ds(lo, n)], RX.at[1, :, pl.ds(lo, n)], peer("gx", 1)),
        ]

    zs = [send(0, PZ, RZ.at[0], peer("gz", -1))]
    if nz > 2:
        zs.append(send(1, PZ, RZ.at[1], peer("gz", 1)))
    ys = exchange_y(2, 0, FIELDS)
    xs = exchange_x(4, 0, FIELDS)
    for c in zs:
        c.wait()
    for s in range(2):
        for x in range(8):
            v = RZ[0, s, x]
            if nz > 2:
                v = jnp.where(lane % 16 < 8, RZ[1, s, x], v)
            E[s, FIELDS, x, 0] = v
    pack_rows(FIELDS, 0)
    ys += exchange_y(8, FIELDS, 1)
    xs += exchange_x(10, FIELDS, 1)
    for c in ys:
        c.wait()
    lax.fori_loop(0, FIELDS + 1, unpack_rows, 0)
    corners = [send(14 + i, SC.at[i], RC.at[i], peer("gx", 2 * i - 1)) for i in range(2)]

    below, above, z_below, z_above = working(8, 256)

    def build(x, _):
        def tiles(s, f):
            t, g = E[s, f, x, 0], swap(E[s, f, x, 1])
            return jnp.where(upper, t, g), jnp.where(upper, g, t)

        for s in range(2):
            strips = tiles(s, FIELDS)
            for f in range(FIELDS):
                pair = tiles(s, f)
                for t in range(2):
                    halo = pltpu.roll(strips[t], 128 - 16 * f - 8, 1)
                    v = jnp.concatenate([pair[t], halo], axis=1)
                    W[7 * s + f, x, t] = v
                    if s == 1:
                        WZ[7 + f, x, t] = z_below(v)
                    elif f < 3:
                        WZ[f, x, t] = z_above(v)
        return 0

    lax.fori_loop(0, 8, build, 0)
    for c in xs + corners:
        c.wait()

    def unpack_planes(f, _):
        for s in range(2):
            for i in range(2):
                v = RX[i, s, f]
                E[s, f, 10 + 2 * i, 0], E[s, f, 11 + 2 * i, 0] = v, swap(v)
                E[s, f, 10 + 2 * i, 1], E[s, f, 11 + 2 * i, 1] = v, v
                v = RC[i, s, f]
                E[s, f, 8 + 6 * i, 1], E[s, f, 9 + 6 * i, 1] = v, swap(v)
        return 0

    lax.fori_loop(0, FIELDS + 1, unpack_planes, 0)
    lax.fori_loop(8, 16, build, 0)

    def before(x):
        return lax.rem(x + 15, 16)

    def after(x):
        return lax.rem(x + 1, 16)

    def pair_of(ref, f, x):
        return ref[f, x, 0], ref[f, x, 1]

    def partner(f, planes, o, tile):
        ref = WZ if o[2] else W
        if o[1]:
            return below(pair_of(ref, f, planes[o[0]]), tile)
        return ref[f, planes[o[0]], tile]

    def bonds(x, _):
        planes = (x, before(x))
        for t in range(2):
            own = [W[3 + k, x, t] for k in range(3)]
            here = W[6, x, t]
            for i, o in enumerate(corner_offsets):
                d = [(0.5 - o[k]) + (partner(10 + k, planes, o, t) - own[k]) for k in range(3)]
                w = here * partner(13, planes, o, t)
                r2 = d[0] * d[0] + d[1] * d[1] + d[2] * d[2]
                inverse = lax.rsqrt(r2)
                stretch = r2 * inverse - bond_length
                J[i, x, t] = w * exchange_scale * jnp.exp(-exchange_decay * stretch)
                P3[i, x, t] = w * jnp.exp(-density_decay * stretch)
                RI[i, x, t] = inverse
        return 0

    lax.fori_loop(0, 16, bonds, 0)

    def upper_bonds(x, _):
        planes = (x, after(x))
        for i, o in enumerate(corner_offsets):
            pair = pair_of(J, i, planes[o[0]])
            if o[2]:
                pair = [z_above(v) for v in pair]
            for t in range(2):
                J1[i, x, t] = above(pair, t) if o[1] else pair[t]
        return 0

    lax.fori_loop(0, 16, upper_bonds, 0)

    def update(u):
        sector = u if u < 8 else 14 - u
        sub, quarter = sector % 2, sector // 2
        tile = quarter // 2
        scale = 0.5 * (step_time if u == 7 else 0.5 * step_time)
        source, target, step = (7, 0, -1) if sub == 0 else (0, 7, 1)
        coupling = J if sub == 0 else J1
        planes = turned_planes()[u]
        shift = below if sub == 0 else above

        @functools.cache
        def around(k, x):
            found = {}
            for oz in range(2):
                pair = pair_of(WZ if oz else W, source + k, x % 16)
                found[0, oz], found[1, oz] = pair[tile], shift(pair, tile)
            return found

        def cross(a, b):
            return [a[1] * b[2] - a[2] * b[1], a[2] * b[0] - a[0] * b[2], a[0] * b[1] - a[1] * b[0]]

        for x in planes:
            c = [coupling[i, x % 16, tile] for i in range(8)]
            h = []
            for k in range(3):
                total = field[k]
                for i, o in enumerate(corner_offsets):
                    total = total + c[i] * around(k, x + step * o[0])[o[1], o[2]]
                h.append(total * scale)
            s = [W[target + k, x % 16, tile] for k in range(3)]
            once = cross(h, s)
            twice = cross(h, once)
            factor = 2.0 / (1.0 + (h[0] * h[0] + h[1] * h[1] + h[2] * h[2]))
            for k in range(3):
                v = s[k] + factor * (once[k] + twice[k])
                W[target + k, x % 16, tile] = v
                WZ[target + k, x % 16, tile] = z_above(v) if sub == 0 else z_below(v)

    for u in range(15):
        update(u)

    def slope(rho):
        return -0.5 * lax.rsqrt(1.0 + rho)

    def slopes(n, _):
        x = lax.rem(n + 15, 16)
        planes = (x, after(x))
        for t in range(2):
            FS[0, x, t] = slope(functools.reduce(jnp.add, [P3[i, x, t] for i in range(8)]))
        rows = []
        for oy in range(2):
            total = []
            for t in range(2):
                flat = P3[2 * oy, planes[0], t] + P3[4 + 2 * oy, planes[1], t]
                high = P3[2 * oy + 1, planes[0], t] + P3[5 + 2 * oy, planes[1], t]
                total.append(flat + z_above(high))
            rows.append(total)
        for t in range(2):
            v = slope(rows[0][t] + above(rows[1], t))
            FS[1, x, t] = v
            FZ[x, t] = z_below(v)
        return 0

    lax.fori_loop(0, 10, slopes, 0)

    def slope_partner(planes, o, tile):
        x = planes[o[0]]
        pair = (FZ[x, 0], FZ[x, 1]) if o[2] else (FS[1, x, 0], FS[1, x, 1])
        return below(pair, tile) if o[1] else pair[tile]

    def forces(x, _):
        planes = (x, before(x))
        sums = [[None] * 2 for _ in range(3)]
        parts = {}
        for t in range(2):
            own = [W[3 + k, x, t] for k in range(3)]
            spins = [W[k, x, t] for k in range(3)]
            mine = FS[0, x, t]
            for i, o in enumerate(corner_offsets):
                d = [(0.5 - o[k]) + (partner(10 + k, planes, o, t) - own[k]) for k in range(3)]
                align = functools.reduce(jnp.add, [spins[k] * partner(7 + k, planes, o, t) for k in range(3)])
                p = P3[i, x, t]
                g = (-pair_decay * pair_scale * (p * p) - density_decay * p * (mine + slope_partner(planes, o, t))
                     + exchange_decay * J[i, x, t] * align) * RI[i, x, t]
                for k in range(3):
                    v = g * d[k]
                    parts[i, t, k] = v
                    sums[k][t] = v if sums[k][t] is None else sums[k][t] + v
        for k in range(3):
            for t in range(2):
                ACC[k, x, t] = sums[k][t]
            for ox in range(2):
                rows = [[parts[4 * ox + 2 * oy, t, k] + z_above(parts[4 * ox + 2 * oy + 1, t, k]) for t in range(2)]
                        for oy in range(2)]
                for t in range(2):
                    v = rows[0][t] + above(rows[1], t)
                    if ox == 0:
                        ACC[3 + k, x, t] = -v
                    else:
                        ACC[3 + k, planes[1], t] = ACC[3 + k, planes[1], t] - v
        return 0

    lax.fori_loop(0, 9, forces, 0)

    def write(x, _):
        for f in range(6):
            for ref, at, out in ((W, 7 * (f // 3) + f % 3, out_s), (ACC, f, out_f)):
                a, b = ref[at, x, 0], ref[at, x, 1]
                out[f // 3, f % 3, x] = jnp.where(upper, a[:, :128], b[:, :128])
        return 0

    lax.fori_loop(0, 8, write, 0)


def on_device(sizes, spin_vectors, displacement, occupied, applied_field):
    vmem = pl.BlockSpec(memory_space=pltpu.VMEM)
    smem = pl.BlockSpec(memory_space=pltpu.SMEM)
    shape = jax.ShapeDtypeStruct(spin_vectors.shape, jnp.float32)

    def buffer(*lead):
        return pltpu.VMEM(lead + (8, 128), jnp.float32)

    def wide(*lead):
        return pltpu.VMEM(lead + (16, 2, 8, 256), jnp.float32)

    return pl.pallas_call(
        functools.partial(kernel, sizes),
        out_shape=(shape, shape),
        in_specs=[vmem, vmem, vmem, smem],
        out_specs=(vmem, vmem),
        scratch_shapes=[
            buffer(2, FIELDS + 1, 16, 2),
            buffer(2, 8), buffer(2, 2, 8),
            buffer(FIELDS + 1, 5), buffer(FIELDS + 1, 5),
            buffer(FIELDS + 1, 6), buffer(FIELDS + 1, 6),
            buffer(2, 2, FIELDS + 1), buffer(2, 2, FIELDS + 1),
            buffer(2, 2, FIELDS + 1), buffer(2, 2, FIELDS + 1),
            wide(14), wide(14), wide(8), wide(8), wide(8), wide(8), wide(2), wide(), wide(6),
            pltpu.SemaphoreType.DMA((16,)),
            pltpu.SemaphoreType.DMA((16,)),
        ],
        compiler_params=pltpu.CompilerParams(
            collective_id=0, has_side_effects=True, vmem_limit_bytes=60 * 1024 * 1024),
    )(spin_vectors, displacement, occupied, applied_field)


def solution(mesh):
    sizes = tuple(mesh.shape[a] for a in axes)
    block = P(None, None, "gx", "gy", "gz")
    return jax.shard_map(
        functools.partial(on_device, sizes),
        mesh=mesh,
        in_specs=(block, block, P(None, "gx", "gy", "gz"), P()),
        out_specs=(block, block),
        check_vma=False,
    )
```

time: 48.7 us -> 34.7 us (0.71)
  Pallas kernels: 45.6 us -> 31.5 us
    pallas_call x1, Pallas kernels: 45.6 us -> 31.5 us  [on_device(): pl.pallas_call(functools.partial(kernel, sizes), out_shape=(shape, shape)...]
where the time goes in v2:
time: 34.7 us; the launch traced here: 34.5 us
  Pallas kernels  31.5 us (91%)
  local copies, waits for them, and re-layouts  2.34 us (7%)
  between operations  0.65 us (2%)
    pallas_call x1, Pallas kernels, on_device(): pl.pallas_call(functools.partial(kernel, sizes), out_shape=(shape, shape)...  31.5 us
    unnamed x4, local copies, waits for them, and re-layouts  2.34 us

profile of v2, /device:TPU:1, one launch (start us, length us, event | category | flops | bytes accessed | tf_op | source)
XLA Modules:
  0.0 34.5 jit_solution(8096257786852766718)
XLA Ops:
  0.6 31.5 %shard_map.59 = (f32[2,3,8,8,128]{4,3,2,1,0:T(8,128)}, f32[2,3,8,8,128]{4,3,2,1,0:T(8,128)}) custom-call(f32[2,3,8,8,128]{4,3,2,1,0:T(8,128)} %spin.1, f32[2,3,8,8,128]{4,3,2,1,0:T(8,128)} %disp.1, s32[2,8,8,128]{3,2,1,0:T(8,128)} %occ.1, f32[3]{0:T(128)} %field.1), custom_call_target="tpu_custom_call" | custom-call | tf_op jit(solution)/shard_map/pallas_call | solution.py:404
  32.2 0.0 copy-start
  32.2 1.7 %copy.8 = f32[2,3,8,8,128]{4,3,2,1,0:T(8,128)} copy(f32[2,3,8,8,128]{4,3,2,1,0:T(8,128)} %get-tuple-element.4) | data formatting | bytes 393216
  33.8 0.0 copy-done
  33.8 0.7 %copy.9 = f32[2,3,8,8,128]{4,3,2,1,0:T(8,128)} copy(f32[2,3,8,8,128]{4,3,2,1,0:T(8,128)S(1)} %copy-done) | data formatting | bytes 393216
Async XLA Ops:
  32.2 1.7 %copy-start = (f32[2,3,8,8,128]{4,3,2,1,0:T(8,128)S(1)}, f32[2,3,8,8,128]{4,3,2,1,0:T(8,128)}, u32[]{:S(2)}) copy-start(f32[2,3,8,8,128]{4,3,2,1,0:T(8,128)} %get-tuple-element.5) | copy-start | bytes 589828

commit v3 on v2

--- a/solution.py
+++ b/solution.py
@@ -19,7 +19,21 @@
 axes = ("gx", "gy", "gz")
 MESH = pl.DeviceIdType.MESH
 
-FIELDS = 7
+DISPLACED, SPUN = 0, 1
+GROUPS = ((0, 4), (9, 3))
+ARRAYS = 16
+
+
+def fields_of(group):
+    first, n = GROUPS[group]
+    return [(first + n * s + f, 7 * s + f + (3 if group == DISPLACED else 0), s) for s in range(2) for f in range(n)]
+
+
+def strip_of(group):
+    first, n = GROUPS[group]
+    return first + 2 * n
+
+
 TO_BELOW = tuple(
     [(i // 4, i, 0, 2, 2 * (i % 4)) for i in range(8)] + [(2, 2 + i, 2, 2, 2 * i) for i in range(4)])
 TO_ABOVE_0 = tuple([(0, i, 7, 1, i) for i in range(8)] + [(1, 2 + i, 5, 2, 2 * i) for i in range(4)])
@@ -71,6 +85,21 @@
     return below, above, z_below, z_above
 
 
+def place_rows():
+    up, down, at, n_up, n_down = [], [], [], 0, 0
+    for group in (DISPLACED, SPUN):
+        for s in [s for _, _, s in fields_of(group)] + [1]:
+            up.append(n_up)
+            down.append(n_down)
+            at.append(s)
+            n_up += 2 + s
+            n_down += 3
+    return up + [n_up], down + [n_down], at
+
+
+UP, DOWN, GEOMETRY = place_rows()
+
+
 def kernel(sizes, spin, disp, occ, field, out_s, out_f, E, PZ, RZ, SU, RU, SD, RD, SX, RX, SC, RC, W, WZ, J, J1, P3, RI, FS, FZ, ACC,
            send_sem, recv_sem):
     nx, ny, nz = sizes
@@ -98,54 +127,56 @@
         return pltpu.roll(v, 4, 0)
 
     def load_own(x, _):
-        for s in range(2):
+        for group in (DISPLACED, SPUN):
             packed = jnp.zeros((8, 128), jnp.float32)
-            for f in range(FIELDS):
+            for n, (e, w, s) in enumerate(fields_of(group)):
+                f = w % 7
                 if f < 3:
                     v = spin[s, f, x]
                 elif f < 6:
                     v = disp[s, f - 3, x]
                 else:
                     v = occ[s, x].astype(jnp.float32)
-                E[s, f, x, 0] = v
-                packed = jnp.where(lane // 16 == f, pltpu.roll(v, 8 + 16 * f, 1), packed)
-            PZ[s, x] = packed
-        return 0
-
-    lax.fori_loop(0, 8, load_own, 0)
+                E[e, x, 0] = v
+                packed = jnp.where(lane // 16 == n, pltpu.roll(v, (8 + 16 * n) % 128, 1), packed)
+            PZ[group, x] = packed
+        return 0
+
+    lax.fori_loop(0, 8, load_own, 0, unroll=2)
     inner = (row >= 2) & (row < 6)
 
-    def routes(s):
-        return ((SU, RU, (0, 2)[s], (TO_ABOVE_0, TO_ABOVE_1)[s]), (SD, RD, 3 * s, TO_BELOW))
-
-    def pack_rows(f, _):
-        for s in range(2):
-            own = [E[s, f, x, 0] for x in range(8)]
-            for out, _unused, first, pieces in routes(s):
-                tiles = {}
-                for tile, x, low, n, to in pieces:
-                    v = pltpu.roll(own[x], (to - low) % 8, 0)
-                    tiles[tile] = jnp.where(row < to, tiles[tile], v) if to else v
-                for tile, v in tiles.items():
-                    out[f, first + tile] = v
-            SX[0, s, f] = jnp.where(inner, own[2], swap(own[3]))
-            SX[1, s, f] = jnp.where(inner, own[4], swap(own[5]))
-        return 0
-
-    def unpack_rows(f, _):
-        for s in range(2):
-            rows = [jnp.zeros((8, 128), jnp.float32)] * 8
-            for _unused, arrived, first, pieces in routes(s):
-                for tile, x, low, n, to in pieces:
-                    v = pltpu.roll(arrived[f, first + tile], (low - to) % 8, 0)
-                    rows[x] = jnp.where((row >= low) & (row < low + n), v, rows[x])
-            for x in range(8):
-                E[s, f, x, 1] = rows[x]
-            SC[0, s, f] = jnp.where(inner, swap(rows[1]), rows[0])
-            SC[1, s, f] = jnp.where(inner, swap(rows[7]), rows[6])
-        return 0
-
-    lax.fori_loop(0, FIELDS, pack_rows, 0)
+    def routes(e):
+        return ((SU, RU, UP[e], (TO_ABOVE_0, TO_ABOVE_1)[GEOMETRY[e]]), (SD, RD, DOWN[e], TO_BELOW))
+
+    def pack_rows(e):
+        own = [E[e, x, 0] for x in range(8)]
+        for out, _unused, first, pieces in routes(e):
+            tiles = {}
+            for tile, x, low, n, to in pieces:
+                v = pltpu.roll(own[x], (to - low) % 8, 0)
+                tiles[tile] = jnp.where(row < to, tiles[tile], v) if to else v
+            for tile, v in tiles.items():
+                out[first + tile] = v
+        SX[0, e] = jnp.where(inner, own[2], swap(own[3]))
+        SX[1, e] = jnp.where(inner, own[4], swap(own[5]))
+
+    def unpack_rows(e):
+        rows = [jnp.zeros((8, 128), jnp.float32)] * 8
+        for _unused, arrived, first, pieces in routes(e):
+            for tile, x, low, n, to in pieces:
+                v = pltpu.roll(arrived[first + tile], (low - to) % 8, 0)
+                rows[x] = jnp.where((row >= low) & (row < low + n), v, rows[x])
+        for x in range(8):
+            E[e, x, 1] = rows[x]
+        SC[0, e] = jnp.where(inner, swap(rows[1]), rows[0])
+        SC[1, e] = jnp.where(inner, swap(rows[7]), rows[6])
+
+    def arrays_of(group):
+        return range(GROUPS[group][0], strip_of(group) + 1)
+
+    for group in (DISPLACED, SPUN):
+        for e, _, _ in fields_of(group):
+            pack_rows(e)
     pl.semaphore_wait(barrier, len(peers))
 
     def send(i, src, dst, to):
@@ -155,81 +186,96 @@
         c.start()
         return c
 
-    def exchange_y(i, lo, n):
+    def exchange_y(i, lo, hi):
+        up = pl.ds(UP[lo], UP[hi] - UP[lo])
+        down = pl.ds(DOWN[lo], DOWN[hi] - DOWN[lo])
         return [
-            send(i, SD.at[pl.ds(lo, n)], RD.at[pl.ds(lo, n)], peer("gy", -1)),
-            send(i + 1, SU.at[pl.ds(lo, n)], RU.at[pl.ds(lo, n)], peer("gy", 1)),
+            send(i, SD.at[down], RD.at[down], peer("gy", -1)),
+            send(i + 1, SU.at[up], RU.at[up], peer("gy", 1)),
         ]
 
-    def exchange_x(i, lo, n):
+    def exchange_x(i, lo, hi):
+        part = pl.ds(lo, hi - lo)
+
         def plane(x):
-            return E.at[:, pl.ds(lo, n), pl.ds(x, 2), 0]
+            return E.at[part, pl.ds(x, 2), 0]
 
         return [
             send(i, plane(0), plane(8), peer("gx", -1)),
             send(i + 1, plane(6), plane(14), peer("gx", 1)),
-            send(i + 2, SX.at[0, :, pl.ds(lo, n)], RX.at[0, :, pl.ds(lo, n)], peer("gx", -1)),
-            send(i + 3, SX.at[1, :, pl.ds(lo, n)], RX.at[1, :, pl.ds(lo, n)], peer("gx", 1)),
+            send(i + 2, SX.at[0, part], RX.at[0, part], peer("gx", -1)),
+            send(i + 3, SX.at[1, part], RX.at[1, part], peer("gx", 1)),
         ]
 
-    zs = [send(0, PZ, RZ.at[0], peer("gz", -1))]
-    if nz > 2:
-        zs.append(send(1, PZ, RZ.at[1], peer("gz", 1)))
-    ys = exchange_y(2, 0, FIELDS)
-    xs = exchange_x(4, 0, FIELDS)
-    for c in zs:
+    def exchange_z(i, group):
+        found = [send(i, PZ.at[group], RZ.at[0, group], peer("gz", -1))]
+        if nz > 2:
+            found.append(send(i + 1, PZ.at[group], RZ.at[1, group], peer("gz", 1)))
+        return found
+
+    def take_strips(group, copies):
+        for c in copies:
+            c.wait()
+        for x in range(8):
+            v = RZ[0, group, x]
+            if nz > 2:
+                v = jnp.where(lane % 16 < 8, RZ[1, group, x], v)
+            E[strip_of(group), x, 0] = v
+        pack_rows(strip_of(group))
+
+    def corner_copies(i, group):
+        part = pl.ds(GROUPS[group][0], len(arrays_of(group)))
+        return [send(i + n, SC.at[n, part], RC.at[n, part], peer("gx", 2 * n - 1)) for n in range(2)]
+
+    z0 = exchange_z(0, DISPLACED)
+    ys0 = exchange_y(4, GROUPS[0][0], strip_of(0))
+    xs0 = exchange_x(12, GROUPS[0][0], strip_of(0))
+    z1 = exchange_z(2, SPUN)
+    take_strips(DISPLACED, z0)
+    ys0 += exchange_y(6, strip_of(0), strip_of(0) + 1)
+    ys1 = exchange_y(8, GROUPS[1][0], strip_of(1))
+    xs0 += exchange_x(16, strip_of(0), strip_of(0) + 1)
+    xs1 = exchange_x(20, GROUPS[1][0], strip_of(1))
+    take_strips(SPUN, z1)
+    ys1 += exchange_y(10, strip_of(1), strip_of(1) + 1)
+    xs1 += exchange_x(24, strip_of(1), strip_of(1) + 1)
+    for c in ys0:
         c.wait()
-    for s in range(2):
-        for x in range(8):
-            v = RZ[0, s, x]
-            if nz > 2:
-                v = jnp.where(lane % 16 < 8, RZ[1, s, x], v)
-            E[s, FIELDS, x, 0] = v
-    pack_rows(FIELDS, 0)
-    ys += exchange_y(8, FIELDS, 1)
-    xs += exchange_x(10, FIELDS, 1)
-    for c in ys:
-        c.wait()
-    lax.fori_loop(0, FIELDS + 1, unpack_rows, 0)
-    corners = [send(14 + i, SC.at[i], RC.at[i], peer("gx", 2 * i - 1)) for i in range(2)]
+    for e in arrays_of(DISPLACED):
+        unpack_rows(e)
+    corners0 = corner_copies(28, DISPLACED)
 
     below, above, z_below, z_above = working(8, 256)
 
-    def build(x, _):
-        def tiles(s, f):
-            t, g = E[s, f, x, 0], swap(E[s, f, x, 1])
+    def build(group, x, _):
+        def tiles(e):
+            t, g = E[e, x, 0], swap(E[e, x, 1])
             return jnp.where(upper, t, g), jnp.where(upper, g, t)
 
-        for s in range(2):
-            strips = tiles(s, FIELDS)
-            for f in range(FIELDS):
-                pair = tiles(s, f)
-                for t in range(2):
-                    halo = pltpu.roll(strips[t], 128 - 16 * f - 8, 1)
-                    v = jnp.concatenate([pair[t], halo], axis=1)
-                    W[7 * s + f, x, t] = v
-                    if s == 1:
-                        WZ[7 + f, x, t] = z_below(v)
-                    elif f < 3:
-                        WZ[f, x, t] = z_above(v)
-        return 0
-
-    lax.fori_loop(0, 8, build, 0)
-    for c in xs + corners:
-        c.wait()
-
-    def unpack_planes(f, _):
-        for s in range(2):
+        strips = tiles(strip_of(group))
+        for n, (e, w, s) in enumerate(fields_of(group)):
+            pair = tiles(e)
+            for t in range(2):
+                halo = pltpu.roll(strips[t], (128 - 16 * n - 8) % 128, 1)
+                v = jnp.concatenate([pair[t], halo], axis=1)
+                W[w, x, t] = v
+                if s == 1:
+                    WZ[w, x, t] = z_below(v)
+                elif group == SPUN:
+                    WZ[w, x, t] = z_above(v)
+        return 0
+
+    build0 = functools.partial(build, DISPLACED)
+    build1 = functools.partial(build, SPUN)
+
+    def unpack_planes(group):
+        for e in arrays_of(group):
             for i in range(2):
-                v = RX[i, s, f]
-                E[s, f, 10 + 2 * i, 0], E[s, f, 11 + 2 * i, 0] = v, swap(v)
-                E[s, f, 10 + 2 * i, 1], E[s, f, 11 + 2 * i, 1] = v, v
-                v = RC[i, s, f]
-                E[s, f, 8 + 6 * i, 1], E[s, f, 9 + 6 * i, 1] = v, swap(v)
-        return 0
-
-    lax.fori_loop(0, FIELDS + 1, unpack_planes, 0)
-    lax.fori_loop(8, 16, build, 0)
+                v = RX[i, e]
+                E[e, 10 + 2 * i, 0], E[e, 11 + 2 * i, 0] = v, swap(v)
+                E[e, 10 + 2 * i, 1], E[e, 11 + 2 * i, 1] = v, v
+                v = RC[i, e]
+                E[e, 8 + 6 * i, 1], E[e, 9 + 6 * i, 1] = v, swap(v)
 
     def before(x):
         return lax.rem(x + 15, 16)
@@ -262,7 +308,20 @@
                 RI[i, x, t] = inverse
         return 0
 
-    lax.fori_loop(0, 16, bonds, 0)
+    lax.fori_loop(0, 8, build0, 0, unroll=2)
+    lax.fori_loop(1, 8, bonds, 0)
+    for c in xs0 + corners0:
+        c.wait()
+    unpack_planes(DISPLACED)
+    lax.fori_loop(8, 16, build0, 0, unroll=2)
+    for c in ys1:
+        c.wait()
+    for e in arrays_of(SPUN):
+        unpack_rows(e)
+    corners1 = corner_copies(30, SPUN)
+    bonds(0, 0)
+    lax.fori_loop(8, 12, bonds, 0)
+    lax.fori_loop(13, 16, bonds, 0)
 
     def upper_bonds(x, _):
         planes = (x, after(x))
@@ -274,7 +333,13 @@
                 J1[i, x, t] = above(pair, t) if o[1] else pair[t]
         return 0
 
-    lax.fori_loop(0, 16, upper_bonds, 0)
+    lax.fori_loop(0, 16, upper_bonds, 0, unroll=4)
+
+    lax.fori_loop(0, 8, build1, 0, unroll=2)
+    for c in xs1 + corners1:
+        c.wait()
+    unpack_planes(SPUN)
+    lax.fori_loop(8, 16, build1, 0, unroll=2)
 
     def update(u):
         sector = u if u < 8 else 14 - u
@@ -339,7 +404,7 @@
             FZ[x, t] = z_below(v)
         return 0
 
-    lax.fori_loop(0, 10, slopes, 0)
+    lax.fori_loop(0, 10, slopes, 0, unroll=5)
 
     def slope_partner(planes, o, tile):
         x = planes[o[0]]
@@ -387,7 +452,7 @@
                 out[f // 3, f % 3, x] = jnp.where(upper, a[:, :128], b[:, :128])
         return 0
 
-    lax.fori_loop(0, 8, write, 0)
+    lax.fori_loop(0, 8, write, 0, unroll=4)
 
 
 def on_device(sizes, spin_vectors, displacement, occupied, applied_field):
@@ -407,15 +472,15 @@
         in_specs=[vmem, vmem, vmem, smem],
         out_specs=(vmem, vmem),
         scratch_shapes=[
-            buffer(2, FIELDS + 1, 16, 2),
+            buffer(ARRAYS, 16, 2),
             buffer(2, 8), buffer(2, 2, 8),
-            buffer(FIELDS + 1, 5), buffer(FIELDS + 1, 5),
-            buffer(FIELDS + 1, 6), buffer(FIELDS + 1, 6),
-            buffer(2, 2, FIELDS + 1), buffer(2, 2, FIELDS + 1),
-            buffer(2, 2, FIELDS + 1), buffer(2, 2, FIELDS + 1),
+            buffer(UP[-1]), buffer(UP[-1]),
+            buffer(DOWN[-1]), buffer(DOWN[-1]),
+            buffer(2, ARRAYS), buffer(2, ARRAYS),
+            buffer(2, ARRAYS), buffer(2, ARRAYS),
             wide(14), wide(14), wide(8), wide(8), wide(8), wide(8), wide(2), wide(), wide(6),
-            pltpu.SemaphoreType.DMA((16,)),
-            pltpu.SemaphoreType.DMA((16,)),
+            pltpu.SemaphoreType.DMA((32,)),
+            pltpu.SemaphoreType.DMA((32,)),
         ],
         compiler_params=pltpu.CompilerParams(
             collective_id=0, has_side_effects=True, vmem_limit_bytes=60 * 1024 * 1024),

time: 34.7 us -> 30.1 us (0.87)
  Pallas kernels: 31.5 us -> 27 us
    pallas_call x1, Pallas kernels: 31.5 us -> 27 us  [on_device(): pl.pallas_call(functools.partial(kernel, sizes), out_shape=(shape, shape)...]
where the time goes in v3:
time: 30.1 us; the launch traced here: 29.9 us
  Pallas kernels  27 us (90%)
  local copies, waits for them, and re-layouts  2.34 us (8%)
  between operations  0.65 us (2%)
    pallas_call x1, Pallas kernels, on_device(): pl.pallas_call(functools.partial(kernel, sizes), out_shape=(shape, shape)...  27 us
    unnamed x4, local copies, waits for them, and re-layouts  2.34 us

profile of v3, /device:TPU:1, one launch (start us, length us, event | category | flops | bytes accessed | tf_op | source)
XLA Modules:
  0.0 29.9 jit_solution(3230827189218437868)
XLA Ops:
  0.6 27.0 %shard_map.59 = (f32[2,3,8,8,128]{4,3,2,1,0:T(8,128)}, f32[2,3,8,8,128]{4,3,2,1,0:T(8,128)}) custom-call(f32[2,3,8,8,128]{4,3,2,1,0:T(8,128)} %spin.1, f32[2,3,8,8,128]{4,3,2,1,0:T(8,128)} %disp.1, s32[2,8,8,128]{3,2,1,0:T(8,128)} %occ.1, f32[3]{0:T(128)} %field.1), custom_call_target="tpu_custom_call" | custom-call | tf_op jit(solution)/shard_map/pallas_call | solution.py:469
  27.6 0.0 copy-start
  27.6 1.7 %copy.8 = f32[2,3,8,8,128]{4,3,2,1,0:T(8,128)} copy(f32[2,3,8,8,128]{4,3,2,1,0:T(8,128)} %get-tuple-element.4) | data formatting | bytes 393216
  29.3 0.0 copy-done
  29.3 0.7 %copy.9 = f32[2,3,8,8,128]{4,3,2,1,0:T(8,128)} copy(f32[2,3,8,8,128]{4,3,2,1,0:T(8,128)S(1)} %copy-done) | data formatting | bytes 393216
Async XLA Ops:
  27.6 1.7 %copy-start = (f32[2,3,8,8,128]{4,3,2,1,0:T(8,128)S(1)}, f32[2,3,8,8,128]{4,3,2,1,0:T(8,128)}, u32[]{:S(2)}) copy-start(f32[2,3,8,8,128]{4,3,2,1,0:T(8,128)} %get-tuple-element.5) | copy-start | bytes 589828
